TPU v7x, 32 devices: a whole 2x2x4 slice. The times are simulated.
32 devices in a mesh: expert: 16 (over z, y, x), half: 2 (over core).
Axes of the slice: x: 2, y: 2, z: 4, core: 2. Of those that a mesh axis runs over, the one named last changes fastest.
Arguments:
- tokens: bfloat16 [1024, 2048], P('expert'), may hold values from -6 to 6
- routes: int32 [1024, 8], P('expert'), may hold values from 0 to 15, all different within a row; in each aligned block of 64 rows (0 to 63, 64 to 127, ...) at most 64 rows name the same one
- gates: float32 [1024, 8], P('expert'), may hold values from 0.05 to 0.5
- cotangent: bfloat16 [1024, 2048], P('expert'), may hold values from -1.5 to 1.5
- w_gate: bfloat16 [16, 2048, 768], P('expert', None, 'half'), may hold values from -0.125 to 0.125
- w_up: bfloat16 [16, 2048, 768], P('expert', None, 'half'), may hold values from -0.125 to 0.125
- w_down: bfloat16 [16, 768, 2048], P('expert', 'half'), may hold values from -0.21875 to 0.21875
Outputs:
- mixed: bfloat16 [1024, 2048], P('expert')
- token_grad: bfloat16 [1024, 2048], P('expert')
- gate_grad: float32 [1024, 8], P('expert')
- grad_gate: bfloat16 [16, 2048, 768], P('expert', None, 'half')
- grad_up: bfloat16 [16, 2048, 768], P('expert', None, 'half')
- grad_down: bfloat16 [16, 768, 2048], P('expert', 'half')
Inputs may be any that keep to these rules, and one draw needn't show every extreme that they name: `routes`: each token names 8 different experts. Among the 64 tokens of one index of the expert axis, no expert is named more than 64 times, a bound that some block reaches.
All inputs are finite; a program needn't handle non-finite values.
Results may differ from a plain program's by a relative error of at most 0.0064.
Values may be sent and summed in bfloat16 or wider, within the bound.
No kernel may reach another device: no remote copies, remote signals or barrier semaphores. Data moves between devices by JAX's collectives and lax.ppermute only.
A program may use at most 128 MiB of HBM per device.

v0:
```python
import jax
import jax.numpy as jnp
from jax import lax
from jax.sharding import PartitionSpec as P


def contract(left, right, left_dim, right_dim):
    return lax.dot_general(
        left, right, (((left_dim,), (right_dim,)), ((), ())), preferred_element_type=jnp.float32
    )


def body(tokens, routes, gates, cotangent, w_gate, w_up, w_down):
    token_count, features = tokens.shape
    top_k = routes.shape[1]
    senders = lax.axis_size("expert")
    halves = lax.axis_size("half")
    experts = w_gate.shape[0] * senders
    slot_count = token_count * top_k
    capacity = 2 * slot_count // experts
    routed = routes.reshape(slot_count)
    onehot = (routed[:, None] == jnp.arange(experts, dtype=jnp.int32)[None, :]).astype(jnp.int32)
    placed = jnp.sum((jnp.cumsum(onehot, axis=0) - onehot) * onehot, axis=1)
    target = routed * capacity + placed
    slot_table = jnp.full((experts * capacity,), slot_count, jnp.int32)
    slot_table = slot_table.at[target].set(jnp.arange(slot_count, dtype=jnp.int32))
    present = slot_table < slot_count
    clipped = jnp.minimum(slot_table, slot_count - 1)
    owners = clipped // top_k
    picked = tokens[owners]
    rows_send = jnp.where(present[:, None], picked, jnp.zeros_like(picked)).reshape(
        experts, capacity, features
    )
    weighted = gates.reshape(slot_count)[clipped][:, None] * cotangent[owners].astype(jnp.float32)
    scaled_send = (
        jnp.where(present[:, None], weighted, 0.0)
        .astype(jnp.bfloat16)
        .reshape(experts, capacity, features)
    )
    half_width = features // halves
    offset = lax.axis_index("half") * half_width
    rows_part = lax.dynamic_slice_in_dim(rows_send, offset, half_width, 2)
    scaled_part = lax.dynamic_slice_in_dim(scaled_send, offset, half_width, 2)
    rows_moved, scaled_moved = (
        lax.all_to_all(rows_part, "expert", split_axis=0, concat_axis=0, tiled=True),
        lax.all_to_all(scaled_part, "expert", split_axis=0, concat_axis=0, tiled=True),
    )
    rows_in, scaled_in = (
        lax.all_gather(rows_moved, "half", axis=2, tiled=True),
        lax.all_gather(scaled_moved, "half", axis=2, tiled=True),
    )
    received = senders * capacity
    rows_in = rows_in.reshape(received, features)
    scaled_in = scaled_in.reshape(received, features)
    wgate = w_gate[0]
    wupper = w_up[0]
    wdown = w_down[0]
    pre_gate = jnp.dot(rows_in, wgate, preferred_element_type=jnp.float32)
    pre_up = jnp.dot(rows_in, wupper, preferred_element_type=jnp.float32)
    sigma = jax.nn.sigmoid(pre_gate)
    hidden = (pre_gate * sigma * pre_up).astype(jnp.bfloat16)
    out_part = jnp.dot(hidden, wdown, preferred_element_type=jnp.float32)
    back_hidden = contract(scaled_in, wdown, 1, 1)
    d_up = (back_hidden * pre_gate * sigma).astype(jnp.bfloat16)
    d_gate = (back_hidden * pre_up * sigma * (1.0 + pre_gate * (1.0 - sigma))).astype(jnp.bfloat16)
    grad_part = contract(d_gate, wgate, 1, 1) + contract(d_up, wupper, 1, 1)
    grad_gate = contract(rows_in, d_gate, 0, 0).astype(jnp.bfloat16)[None]
    grad_up = contract(rows_in, d_up, 0, 0).astype(jnp.bfloat16)[None]
    grad_down = contract(hidden, scaled_in, 0, 0).astype(jnp.bfloat16)[None]
    out_mine, grad_mine = (
        lax.psum_scatter(out_part, "half", scatter_dimension=1, tiled=True),
        lax.psum_scatter(grad_part, "half", scatter_dimension=1, tiled=True),
    )
    out_mine = out_mine.astype(jnp.bfloat16)
    grad_mine = grad_mine.astype(jnp.bfloat16)
    out_block = out_mine.reshape(senders, capacity, features // halves)
    grad_block = grad_mine.reshape(senders, capacity, features // halves)
    out_back, grad_back = (
        lax.all_to_all(out_block, "expert", split_axis=0, concat_axis=0, tiled=True),
        lax.all_to_all(grad_block, "expert", split_axis=0, concat_axis=0, tiled=True),
    )
    out_home, grad_home = (
        lax.all_gather(out_back, "half", axis=2, tiled=True),
        lax.all_gather(grad_back, "half", axis=2, tiled=True),
    )
    out_slots = out_home.reshape(experts * capacity, features)[target].reshape(
        token_count, top_k, features
    )
    grad_slots = grad_home.reshape(experts * capacity, features)[target].reshape(
        token_count, top_k, features
    )
    out_float = out_slots.astype(jnp.float32)
    mixed = jnp.sum(gates[:, :, None] * out_float, axis=1).astype(jnp.bfloat16)
    gate_grad = jnp.sum(cotangent.astype(jnp.float32)[:, None, :] * out_float, axis=2)
    token_grad = jnp.sum(grad_slots.astype(jnp.float32), axis=1).astype(jnp.bfloat16)
    return (mixed, token_grad, gate_grad, grad_gate, grad_up, grad_down)


def solution(mesh):
    placed = (
        P("expert", None),
        P("expert", None),
        P("expert", None),
        P("expert", None),
        P("expert", None, "half"),
        P("expert", None, "half"),
        P("expert", "half", None),
    )
    return jax.shard_map(
        body,
        mesh=mesh,
        in_specs=placed,
        out_specs=(
            P("expert", None),
            P("expert", None),
            P("expert", None),
            P("expert", None, "half"),
            P("expert", None, "half"),
            P("expert", "half", None),
        ),
        check_vma=False,
    )
```

profile of v0, /device:TPU:0, one launch (start us, length us, event | category | flops | bytes accessed | tf_op | source)
XLA Modules:
  0.0 336.4 jit_solution(8141604444194219002)
XLA Ops:
  7.2 0.8 broadcast_multiply_fusion
  8.0 0.8 copy.22
  8.8 0.1 eq.29
  8.9 0.1 eq.25
  9.0 0.1 copy.21
  9.1 0.1 mul.80
  9.2 1.2 reduce-window.6
  10.3 0.2 slice_reduce_fusion
  10.6 0.1 fusion.20
  10.7 2.4 scatter_custom_fusion
  13.2 0.1 broadcast_in_dim.48
  13.3 6.0 %gather_fusion = bf16[1024,2048]{1,0:T(8,128)(2,1)} fusion(bf16[64,2048]{1,0:T(8,128)(2,1)S(1)} %copy-done.2, s32[1024]{0:T(1024)S(1)} %get-tuple-element.18), kind=kCustom, calls=%fused_computation | custom fusion | bytes 8392704 | tf_op jit(solution)/shard_map/gather | solution.py:30
  19.2 3.4 %dynamic-slice_select_fusion = bf16[16,64,1024]{2,1,0:T(8,128)(2,1)} fusion(bf16[16,64,2048]{2,1,0:T(8,128)(2,1)} %bitcast.75, s32[]{:T(128)S(6)} %select_n.42, pred[16,64]{1,0:T(8,128)(4,1)S(1)} %broadcast_in_dim.48), kind=kLoop, calls=%fused_computation.20 | loop fusion | flops 1048576 | bytes 4195332 | tf_op jit(solution)/shard_map/jit(_where)/select_n | solution.py:31
  22.6 8.5 %all-to-all-start = ((bf16[16,64,1024]{2,1,0:T(8,128)(2,1)}), bf16[16,64,1024]{2,1,0:T(8,128)(2,1)}, u32[]{:S(2)}, u32[]{:S(2)}) async-start(bf16[16,64,1024]{2,1,0:T(8,128)(2,1)} %dynamic-slice_select_fusion), calls=%async_computation | async-start | bytes 4194304 | tf_op jit(solution)/shard_map/all_to_all | solution.py:45
  31.2 0.1 copy.20
  31.3 0.1 reshape.123
  31.4 6.9 %gather_fusion.2 = f32[1024]{0:T(1024)S(1)} fusion(f32[512]{0:T(512)S(1)} %reshape.123, s32[1024]{0:T(1024)S(1)} %get-tuple-element.17), kind=kCustom, calls=%fused_computation.2 | custom fusion | bytes 12288 | tf_op jit(solution)/shard_map/gather | solution.py:34
  38.3 0.1 mul.86
  38.4 6.0 %gather_fusion.3 = bf16[1024,2048]{1,0:T(8,128)(2,1)} fusion(bf16[64,2048]{1,0:T(8,128)(2,1)S(1)} %copy-done.1, s32[1024]{0:T(1024)S(1)} %get-tuple-element.18), kind=kCustom, calls=%fused_computation.3 | custom fusion | bytes 8392704 | tf_op jit(solution)/shard_map/gather | solution.py:34
  44.3 29.9 %all-to-all-done = bf16[16,64,1024]{2,1,0:T(8,128)(2,1)} async-done(((bf16[16,64,1024]{2,1,0:T(8,128)(2,1)}), bf16[16,64,1024]{2,1,0:T(8,128)(2,1)}, u32[]{:S(2)}, u32[]{:S(2)}) %all-to-all-start) | async-done | bytes 2097184 | tf_op jit(solution)/shard_map/all_to_all | solution.py:45
  74.3 0.0 all-gather.9.cloned.1.call-start
  74.3 2.2 fusion.3
  76.5 58.1 %all_to_all.20 = bf16[16,64,1024]{2,1,0:T(8,128)(2,1)} all-to-all(bf16[16,64,1024]{2,1,0:T(8,128)(2,1)S(1)} %fusion.3), channel_id=1, replica_groups=mesh['expert'=16,'half'=2] {'expert'}, dimensions={0} | all-to-all | bytes 4194304 | tf_op jit(solution)/shard_map/all_to_all | solution.py:46
  134.6 0.2 reduce-scatter.5.cloned.1.call-start
  134.9 6.3 %fusion.12 = f32[1024,384]{1,0:T(8,128)} fusion(bf16[1024,2048]{1,0:T(8,128)(2,1)} %bitcast.81, bf16[1,2048,384]{2,1,0:T(8,128)(2,1)} %param.12), kind=kOutput, calls=%fused_computation.27 | convolution fusion | flops 1610612736 | bytes 7340032 | tf_op jit(solution)/shard_map/dot_general | solution.py:59
  141.2 3.5 %fusion.16 = f32[1024,384]{1,0:T(8,128)} fusion(bf16[1024,2048]{1,0:T(8,128)(2,1)S(1)} %bitcast.82, bf16[1,2048,384]{2,1,0:T(8,128)(2,1)S(1)} %copy-done.3), kind=kOutput, calls=%fused_computation.31 | convolution fusion | flops 1610612736 | bytes 7340032 | tf_op jit(solution)/shard_map/dot_general | solution.py:58
  144.7 2.1 all-gather.9.cloned.1.call-done
  146.8 6.9 %multiply_convert_fusion = (bf16[1024,384]{1,0:T(8,128)(2,1)S(1)}, bf16[1024,384]{1,0:T(8,128)(2,1)S(1)}, bf16[1024,384]{1,0:T(8,128)(2,1)}) fusion(f32[1024,384]{1,0:T(8,128)} %fusion.16, f32[1024,384]{1,0:T(8,128)} %fusion.12, bf16[1024,2048]{1,0:T(8,128)(2,1)} %bitcast.85, bf16[1,384,2048]{2,1,0:T(8,128)(2,1)S(1)} %copy-done), kind=kOutput, calls=%fused_computation.33 | convolution fusion | flops 1616904192 | bytes 11272192 | tf_op jit(solution)/shard_map/dot_general | solution.py:8
  153.6 2.4 fusion.14
  156.0 5.6 %convolution_add_fusion = f32[1024,2048]{1,0:T(8,128)} fusion(f32[1024,2048]{1,0:T(8,128)S(1)} %fusion.14, bf16[1024,384]{1,0:T(8,128)(2,1)S(1)} %get-tuple-element.14, bf16[1,2048,384]{2,1,0:T(8,128)(2,1)S(1)} %copy-done.4), kind=kOutput, calls=%fused_computation.8 | convolution fusion | flops 1612709888 | bytes 19136512 | tf_op jit(solution)/shard_map/dot_general | solution.py:8
  161.7 0.0 reduce-scatter.3.cloned.1.call-start
  161.7 1.1 copy-done.9
  162.8 5.6 %fusion.9 = f32[1024,2048]{1,0:T(8,128)} fusion(bf16[1024,384]{1,0:T(8,128)(2,1)S(1)} %copy-done.9, bf16[1,384,2048]{2,1,0:T(8,128)(2,1)S(1)} %copy-done), kind=kOutput, calls=%fused_computation.24 | convolution fusion | flops 1610612736 | bytes 10747904 | tf_op jit(solution)/shard_map/dot_general | solution.py:62
  168.4 0.0 all-gather.11.cloned.1.call-start
  168.4 10.8 %reduce-scatter.5.cloned.1.call-done = f32[1024,1024]{1,0:T(8,128)} async-done(((f32[1024,2048]{1,0:T(8,128)}), f32[1024,1024]{1,0:T(8,128)}) %reduce-scatter.5.cloned.1.call-update) | async-done | bytes 4194320 | tf_op jit(solution)/shard_map/reduce_scatter | solution.py:72
  179.2 2.5 convert_element_type.72
  181.8 55.9 %all_to_all.21 = bf16[16,64,1024]{2,1,0:T(8,128)(2,1)} all-to-all(bf16[16,64,1024]{2,1,0:T(8,128)(2,1)S(1)} %bitcast.76), channel_id=1, replica_groups=mesh['expert'=16,'half'=2] {'expert'}, dimensions={0} | all-to-all | bytes 4194304 | tf_op jit(solution)/shard_map/all_to_all | solution.py:80
  237.7 0.0 all-gather.7.cloned.1.call-start
  237.8 2.5 convert_element_type.63
  240.3 52.1 %all_to_all.22 = bf16[16,64,1024]{2,1,0:T(8,128)(2,1)} all-to-all(bf16[16,64,1024]{2,1,0:T(8,128)(2,1)S(1)} %bitcast.77), channel_id=1, replica_groups=mesh['expert'=16,'half'=2] {'expert'}, dimensions={0} | all-to-all | bytes 4194304 | tf_op jit(solution)/shard_map/all_to_all | solution.py:79
  292.5 5.3 %fusion.6 = bf16[1,384,2048]{2,1,0:T(8,128)(2,1)} fusion(bf16[1024,384]{1,0:T(8,128)(2,1)S(1)} %copy-done.9, bf16[1024,2048]{1,0:T(8,128)(2,1)} %bitcast.86), kind=kOutput, calls=%fused_computation.19 | convolution fusion | flops 1611399168 | bytes 6553600 | tf_op jit(solution)/shard_map/dot_general | solution.py:8
  297.8 3.6 %fusion.5 = bf16[1,2048,384]{2,1,0:T(8,128)(2,1)} fusion(bf16[1024,2048]{1,0:T(8,128)(2,1)S(1)} %bitcast.83, bf16[1024,384]{1,0:T(8,128)(2,1)S(1)} %copy-done.8), kind=kOutput, calls=%fused_computation.18 | convolution fusion | flops 1611399168 | bytes 6553600 | tf_op jit(solution)/shard_map/dot_general | solution.py:8
  301.4 3.6 %fusion.4 = bf16[1,2048,384]{2,1,0:T(8,128)(2,1)} fusion(bf16[1024,2048]{1,0:T(8,128)(2,1)S(1)} %bitcast.84, bf16[1024,384]{1,0:T(8,128)(2,1)S(1)} %copy-done.6), kind=kOutput, calls=%fused_computation.17 | convolution fusion | flops 1611399168 | bytes 6553600 | tf_op jit(solution)/shard_map/dot_general | solution.py:8
  305.0 8.0 %gather_fusion.4 = bf16[512,2048]{1,0:T(8,128)(2,1)} fusion(bf16[1024,2048]{1,0:T(8,128)(2,1)} %bitcast.72, s32[1024]{0:T(1024)S(1)} %pad_clamp_fusion), kind=kCustom, calls=%fused_computation.4 | custom fusion | bytes 4196352 | tf_op jit(solution)/shard_map/gather | solution.py:89
  312.9 3.7 %bitcast_reduce_fusion = bf16[64,2048]{1,0:T(8,128)(2,1)} fusion(bf16[512,2048]{1,0:T(8,128)(2,1)} %gather_fusion.4), kind=kLoop, calls=%fused_computation.21 | loop fusion | flops 917504 | bytes 2359296 | tf_op jit(solution)/shard_map/reduce_sum | solution.py:95
  316.7 8.3 %gather_fusion.1 = bf16[512,2048]{1,0:T(8,128)(2,1)} fusion(bf16[1024,2048]{1,0:T(8,128)(2,1)} %bitcast.73, s32[1024]{0:T(1024)S(1)} %pad_clamp_fusion), kind=kCustom, calls=%fused_computation.1 | custom fusion | bytes 4196352 | tf_op jit(solution)/shard_map/gather | solution.py:86
  324.9 4.0 %fusion.1 = (f32[64,8]{1,0:T(8,128)S(1)}, bf16[64,2048]{1,0:T(8,128)(2,1)}) fusion(bf16[512,2048]{1,0:T(8,128)(2,1)} %gather_fusion.1, f32[64,2048]{1,0:T(8,128)S(1)} %convert_element_type.73, f32[64,8]{1,0:T(8,128)S(1)} %copy.20), kind=kLoop, calls=%fused_computation.10 | loop fusion | flops 5111296 | bytes 2887680 | tf_op jit(solution)/shard_map/reduce_sum | solution.py:94
  328.9 0.7 copy.26
  (45 shorter events, 0.4 us)
Async XLA Ops:
  7.2 139.6 %copy-start = (bf16[1,384,2048]{2,1,0:T(8,128)(2,1)S(1)}, bf16[1,384,2048]{2,1,0:T(8,128)(2,1)}, u32[]{:S(2)}) copy-start(bf16[1,384,2048]{2,1,0:T(8,128)(2,1)} %param.13) | copy-start | bytes 4718596
  7.2 6.1 %copy-start.2 = (bf16[64,2048]{1,0:T(8,128)(2,1)S(1)}, bf16[64,2048]{1,0:T(8,128)(2,1)}, u32[]{:S(2)}) copy-start(bf16[64,2048]{1,0:T(8,128)(2,1)} %param.7) | copy-start | bytes 786436
  22.6 8.6 %copy-start.10 = (f32[64,8]{0,1:T(8,128)S(1)}, f32[64,8]{0,1:T(8,128)}, u32[]{:S(2)}) copy-start(f32[64,8]{0,1:T(8,128)} %param.9) | copy-start | bytes 6148
  22.6 51.6 %all-to-all-start = ((bf16[16,64,1024]{2,1,0:T(8,128)(2,1)}), bf16[16,64,1024]{2,1,0:T(8,128)(2,1)}, u32[]{:S(2)}, u32[]{:S(2)}) async-start(bf16[16,64,1024]{2,1,0:T(8,128)(2,1)} %dynamic-slice_select_fusion), calls=%async_computation | async-start | bytes 4194304 | tf_op jit(solution)/shard_map/all_to_all | solution.py:45
  31.2 103.7 %all-gather.5.cloned.1.call-start = ((), (), s32[]{:S(2)}) async-start(), calls=%async_computation.6 | async-start | bytes 6291456 | tf_op jit(solution)/shard_map/all_gather | solution.py:49
  31.4 7.0 %copy-start.1 = (bf16[64,2048]{1,0:T(8,128)(2,1)S(1)}, bf16[64,2048]{1,0:T(8,128)(2,1)}, u32[]{:S(2)}) copy-start(bf16[64,2048]{1,0:T(8,128)(2,1)} %param.10) | copy-start | bytes 786436
  74.3 72.5 %all-gather.9.cloned.1.call-start = ((), (), s32[]{:S(2)}) async-start(), calls=%async_computation.9 | async-start | bytes 6291456 | tf_op jit(solution)/shard_map/all_gather | solution.py:50
  134.6 44.6 %reduce-scatter.5.cloned.1.call-start = ((), (), s32[]{:S(2)}) async-start(), calls=%async_computation.10 | async-start | bytes 12582912 | tf_op jit(solution)/shard_map/reduce_scatter | solution.py:72
  134.9 6.3 %copy-start.3 = (bf16[1,2048,384]{2,1,0:T(8,128)(2,1)S(1)}, bf16[1,2048,384]{2,1,0:T(8,128)(2,1)}, u32[]{:S(2)}) copy-start(bf16[1,2048,384]{2,1,0:T(8,128)(2,1)} %param.11) | copy-start | bytes 4718596
  134.9 6.3 %copy-start.11 = (bf16[16,64,2048]{2,1,0:T(8,128)(2,1)S(1)}, bf16[16,64,2048]{2,1,0:T(8,128)(2,1)}, u32[]{:S(2)}) copy-start(bf16[16,64,2048]{2,1,0:T(8,128)(2,1)} %all-gather.5.cloned.1.call-done) | copy-start | bytes 12582916
  153.6 2.4 copy-start.5
  153.6 2.4 copy-start.7
  153.6 2.4 copy-start.4
  161.6 1.1 copy-start.9
  161.7 76.1 %reduce-scatter.3.cloned.1.call-start = ((), (), s32[]{:S(2)}) async-start(), calls=%async_computation.7 | async-start | bytes 12582912 | tf_op jit(solution)/shard_map/reduce_scatter | solution.py:71
  168.4 136.6 %all-gather.11.cloned.1.call-start = ((), (), s32[]{:S(2)}) async-start(), calls=%async_computation.11 | async-start | bytes 6291456 | tf_op jit(solution)/shard_map/all_gather | solution.py:84
  237.7 78.9 %all-gather.7.cloned.1.call-start = ((), (), s32[]{:S(2)}) async-start(), calls=%async_computation.8 | async-start | bytes 6291456 | tf_op jit(solution)/shard_map/all_gather | solution.py:83
  292.5 5.3 %copy-start.8 = (bf16[1024,384]{1,0:T(8,128)(2,1)S(1)}, bf16[1024,384]{1,0:T(8,128)(2,1)}, u32[]{:S(2)}) copy-start(bf16[1024,384]{1,0:T(8,128)(2,1)} %copy-done.7) | copy-start | bytes 2359300
  292.5 5.3 %copy-start.12 = (bf16[16,64,2048]{2,1,0:T(8,128)(2,1)S(1)}, bf16[16,64,2048]{2,1,0:T(8,128)(2,1)}, u32[]{:S(2)}) copy-start(bf16[16,64,2048]{2,1,0:T(8,128)(2,1)} %all-gather.5.cloned.1.call-done) | copy-start | bytes 12582916
  297.8 3.6 %copy-start.6 = (bf16[1024,384]{1,0:T(8,128)(2,1)S(1)}, bf16[1024,384]{1,0:T(8,128)(2,1)}, u32[]{:S(2)}) copy-start(bf16[1024,384]{1,0:T(8,128)(2,1)} %copy-done.5) | copy-start | bytes 2359300
Sparse Core Ops, SparseCore 0:
  74.4 18.0 all-gather.4
  134.8 11.9 all-gather.8
  161.8 17.4 reduce-scatter.4
  181.4 17.5 reduce-scatter.2
  237.8 11.9 all-gather.10
  292.5 11.9 all-gather.6
where the time goes:
time: 337 us; the launch traced here: 336 us
  blocking collectives  166 us (49%)
  waiting for transfers between devices  43 us (13%)
  matrix products  42.6 us (13%)
  local copies, waits for them, and re-layouts  41 us (12%)
  other arithmetic  20.4 us (6%)
  between operations  14.3 us (4%)
  starting transfers between devices  8.96 us (3%)
    all_to_all x1, blocking collectives, body(): lax.all_to_all(scaled_part, 'expert', split_axis=0, concat_axis=0, tiled=...  58.1 us
    all_to_all x1, blocking collectives, body(): lax.all_to_all(grad_block, 'expert', split_axis=0, concat_axis=0, tiled=T...  55.9 us
    all_to_all x1, blocking collectives, body(): lax.all_to_all(out_block, 'expert', split_axis=0, concat_axis=0, tiled=True)  52.1 us
    all_to_all x1, waiting for transfers between devices, body(): lax.all_to_all(rows_part, 'expert', split_axis=0, concat_axis=0, tiled=True)  29.9 us
    dot_general x6, matrix products, contract(): lax.dot_general(left, right, (((left_dim,), (right_dim,)), ((), ())), pre...  27.3 us
    reduce_scatter x1, waiting for transfers between devices, body(): lax.psum_scatter(grad_part, 'half', scatter_dimension=1, tiled=True)  10.8 us
    all_to_all x1, starting transfers between devices, body(): lax.all_to_all(rows_part, 'expert', split_axis=0, concat_axis=0, tiled=True)  8.52 us
    gather x1, local copies, waits for them, and re-layouts, body(): out_home.reshape(experts * capacity, features)[target]  8.25 us
  transfers between devices with their start and end apart: 7, of which 3 were waited for; matrix products, arithmetic and copies ran while one was open for 18% of the time, Pallas kernels for 0%

commit v1 on v0

--- a/solution.py
+++ b/solution.py
@@ -1,6 +1,8 @@
 import jax
 import jax.numpy as jnp
 from jax import lax
+from jax.experimental import pallas as pl
+from jax.experimental.pallas import tpu as pltpu
 from jax.sharding import PartitionSpec as P
 
 
@@ -10,7 +12,7 @@
     )
 
 
-def body(tokens, routes, gates, cotangent, w_gate, w_up, w_down):
+def slot_body(tokens, routes, gates, cotangent, w_gate, w_up, w_down):
     token_count, features = tokens.shape
     top_k = routes.shape[1]
     senders = lax.axis_size("expert")
@@ -96,6 +98,416 @@
     return (mixed, token_grad, gate_grad, grad_gate, grad_up, grad_down)
 
 
+def rolled(n, step):
+    return [((i + 4 * step) % n, i) for i in range(n)]
+
+
+def flipped(n, bit):
+    return [(i, i ^ bit) for i in range(n)]
+
+
+def swap_half(x):
+    return lax.ppermute(x, "half", [(0, 1), (1, 0)])
+
+
+def near_first(groups):
+    return sorted(range(1, groups), key=lambda j: min(j, groups - j))
+
+
+def stack(*parts):
+    return jnp.concatenate(parts, axis=0)
+
+
+COLOURS = ((1, 2), (2, 1))
+
+
+def flip(x, n, bit):
+    return lax.ppermute(x, "expert", flipped(n, bit))
+
+
+def after(x, *earlier):
+    return lax.optimization_barrier((x, *earlier))[0]
+
+
+def spread(block, n):
+    rows = block.shape[0] // 2
+    far_rows = rows * (n // 4 - 1)
+    near_rows = rows + far_rows
+    shifted = [lax.ppermute(block, "expert", rolled(n, j)) for j in near_first(n // 4)]
+    group_one, group_two = [], []
+    for colour, (first, second) in enumerate(COLOURS):
+        base = colour * 2 * near_rows
+        part = slice(colour * rows, (colour + 1) * rows)
+        own = block[part]
+        far = stack(*[s[part] for s in shifted])
+        own_first = flip(own, n, first)
+        own_second = flip(stack(own, own_first), n, second)
+        far_first = flip(far, n, first)
+        far_second = flip(stack(far, far_first), n, second)
+        mid = base + near_rows
+        group_one += [
+            (own, [(base, rows)]),
+            (far, [(base + rows, far_rows)]),
+            (own_first, [(mid, rows)]),
+            (far_first, [(mid + rows, far_rows)]),
+        ]
+        group_two += [
+            (own_second, [(base, rows), (mid, rows)]),
+            (far_second, [(base + rows, far_rows), (mid + rows, far_rows)]),
+        ]
+    return group_one, group_two
+
+
+def narrow(x):
+    return x.astype(jnp.bfloat16)
+
+
+def wide(x):
+    return x.astype(jnp.float32)
+
+
+def shift_home(block, n, j):
+    return lax.ppermute(narrow(block), "expert", [(d, s) for s, d in rolled(n, j)])
+
+
+def by_colour(x):
+    m = x.shape[0] // 2
+    return x[:m], x[m:]
+
+
+def fold(n, kept, sent, which):
+    result = []
+    for bits, mine, gone in zip(COLOURS, kept, sent):
+        moved = flip(narrow(gone), n, bits[which])
+        result.append((mine, moved))
+    return result
+
+
+def summed(pairs):
+    return [mine + wide(moved) for mine, moved in pairs]
+
+
+def collect_outputs(one, two, n, held):
+    rows = one.shape[0] // n
+    near_rows = rows * (n // 4)
+    pairs = fold(n, by_colour(one), by_colour(two), 1)
+    parts = summed([(mine, after(moved, held)) for mine, moved in pairs])
+    runs = [p[at : at + near_rows] for p in parts for at in (0, near_rows)]
+    shifted = []
+    for at, j in enumerate(near_first(n // 4)):
+        block = stack(*[run[(at + 1) * rows : (at + 2) * rows] for run in runs])
+        shifted.append(shift_home(block, n, j))
+    return stack(*[run[:rows] for run in runs]), shifted
+
+
+def finish_outputs(kept, shifted, n, held):
+    total = kept
+    for moved in shifted:
+        total = total + wide(after(moved, held))
+    halves = [by_colour(part) for part in by_colour(total)]
+    return narrow(stack(*summed(fold(n, *zip(*halves), 0))))
+
+
+def collect_gradients(one, two, n):
+    rows = one.shape[0] // n
+    near_rows = rows * (n // 4)
+
+    def far(x):
+        return stack(x[rows:near_rows], x[near_rows + rows :])
+
+    def own(x):
+        return stack(x[:rows], x[near_rows : near_rows + rows])
+
+    ones, twos = by_colour(one), by_colour(two)
+    far_pairs = fold(n, [far(x) for x in ones], [far(x) for x in twos], 1)
+    own_pairs = fold(n, [own(x) for x in ones], [own(x) for x in twos], 1)
+    far_pairs = fold(n, *zip(*[by_colour(x) for x in summed(far_pairs)]), 0)
+    fars = summed(far_pairs)
+    own_pairs = fold(n, *zip(*[by_colour(x) for x in summed(own_pairs)]), 0)
+    mark = own_pairs[1][1]
+    total = stack(*summed(own_pairs))
+    shifted = []
+    for at, j in enumerate(near_first(n // 4)):
+        block = stack(*[part[at * rows : (at + 1) * rows] for part in fars])
+        shifted.append(shift_home(block, n, j))
+    return total, shifted, mark
+
+
+VMEM = pl.BlockSpec(memory_space=pltpu.VMEM)
+SMEM = pl.BlockSpec(memory_space=pltpu.SMEM)
+
+
+def size_of(x):
+    return x.size * x.dtype.itemsize
+
+
+def whole(kernel, out_shapes, args, scalars=0, flops=0):
+    moved = sum(size_of(x) for x in jax.tree.leaves((args, out_shapes)))
+    return pl.pallas_call(
+        kernel,
+        out_shape=out_shapes,
+        in_specs=[SMEM] * scalars + [VMEM] * (len(args) - scalars),
+        out_specs=jax.tree.map(lambda _: VMEM, out_shapes),
+        cost_estimate=pl.CostEstimate(flops=flops, bytes_accessed=moved, transcendentals=0),
+        compiler_params=pltpu.CompilerParams(vmem_limit_bytes=moved + 4 * 2**20),
+    )(*args)
+
+
+def assemble(placed):
+    parts, places = zip(*placed)
+
+    def kernel(*refs):
+        out = refs[-1]
+        for ref, runs in zip(refs[:-1], places):
+            at = 0
+            for start, count in runs:
+                out[start : start + count] = ref[at : at + count]
+                at += count
+
+    total = sum(p.shape[0] for p in parts)
+    shape = jax.ShapeDtypeStruct((total, parts[0].shape[1]), parts[0].dtype)
+    return whole(kernel, shape, parts, 0, 1000 * total)
+
+
+def product_over_rows(left, right, tall=None):
+    groups = len(left)
+    tile = 256
+    rows, width = right[0].shape
+
+    def kernel(*refs):
+        def joined(k):
+            return jnp.concatenate([ref[...] for ref in refs[k * groups : (k + 1) * groups]], 0)
+
+        both = narrow(contract(joined(0), joined(1), 0, 0))
+        outs = refs[2 * groups :]
+        for at, out in enumerate(outs):
+            m = both.shape[1] // len(outs)
+            out[0] = both[:, at * m : (at + 1) * m]
+
+    def fixed(cols):
+        return [pl.BlockSpec((rows, cols), lambda i: (0, 0))] * groups
+
+    def moving():
+        return [pl.BlockSpec((rows, tile), lambda i: (0, i))] * groups
+
+    if tall is None:
+        unit, features = left[0].shape[1], width
+        in_specs = fixed(unit) + moving()
+        out_shape = [jax.ShapeDtypeStruct((1, unit, features), jnp.bfloat16)]
+        out_specs = [pl.BlockSpec((1, unit, tile), lambda i: (0, 0, i))]
+        flops = 2 * groups * rows * unit * features
+    else:
+        unit = width // 2
+        features = tall
+        in_specs = moving() + fixed(width)
+        out_shape = [jax.ShapeDtypeStruct((1, features, unit), jnp.bfloat16)] * 2
+        out_specs = [pl.BlockSpec((1, tile, unit), lambda i: (0, i, 0))] * 2
+        flops = 2 * groups * rows * width * features
+    return pl.pallas_call(
+        kernel,
+        grid=(features // tile,),
+        out_shape=out_shape,
+        in_specs=in_specs,
+        out_specs=out_specs,
+        cost_estimate=pl.CostEstimate(flops=flops, bytes_accessed=0, transcendentals=0),
+        compiler_params=pltpu.CompilerParams(vmem_limit_bytes=14 * 2**20),
+    )(*left, *right)
+
+
+def blocks_of(rows, step, work):
+    def one(i, carry):
+        work(pl.ds(pl.multiple_of(i * step, step), step))
+        return carry
+
+    lax.fori_loop(0, rows // step, one, 0)
+
+
+def gate_of(side, experts, me):
+    lanes = lax.broadcasted_iota(jnp.int32, side.shape, 1)
+    named = (lax.rem(lanes, experts) == me) & (lanes < 3 * experts)
+    return jnp.sum(jnp.where(named, side.astype(jnp.float32), 0.0), axis=1, keepdims=True)
+
+
+def forward(rows_in, w_in, w_down, where, experts, out_dtype):
+    rows = rows_in.shape[0]
+    features, width = w_in.shape
+    unit = width // 2
+
+    def kernel(where_ref, x_ref, win_ref, down_ref, pre_ref, weighted_ref, out_ref):
+        me = where_ref[0]
+
+        def work(at):
+            pre = jnp.dot(
+                x_ref[at, :features], win_ref[...], preferred_element_type=jnp.float32
+            )
+            pre_ref[at, :] = pre
+            gate = gate_of(x_ref[at, features:], experts, me)
+            pre_gate = pre[:, :unit]
+            hidden = pre_gate * jax.nn.sigmoid(pre_gate) * pre[:, unit:]
+            weighted = (gate * hidden).astype(jnp.bfloat16)
+            weighted_ref[at, :] = weighted
+            out_ref[at, :] = jnp.dot(
+                weighted, down_ref[...], preferred_element_type=jnp.float32
+            ).astype(out_dtype)
+
+        blocks_of(rows, min(rows, 256), work)
+
+    shapes = (
+        jax.ShapeDtypeStruct((rows, width), jnp.float32),
+        jax.ShapeDtypeStruct((rows, unit), jnp.bfloat16),
+        jax.ShapeDtypeStruct((rows, features), out_dtype),
+    )
+    return whole(kernel, shapes, (where, rows_in, w_in, w_down), 1, 3 * rows * features * width)
+
+
+def backward(cot, rows_in, pre, w_in, w_down, where, experts, halves, out_dtype):
+    rows, features = cot.shape
+    width = w_in.shape[1]
+    unit = width // 2
+    back_width = -(-3 * halves * experts // 128) * 128
+
+    def kernel(where_ref, cot_ref, side_ref, pre_ref, win_ref, down_ref, d_ref, out_ref):
+        me, half = where_ref[0], where_ref[1]
+
+        def work(at):
+            back = lax.dot_general(
+                cot_ref[at, :],
+                down_ref[...],
+                (((1,), (1,)), ((), ())),
+                preferred_element_type=jnp.float32,
+            )
+            gate = gate_of(side_ref[at, features:], experts, me)
+            pre_gate, pre_up = pre_ref[at, :unit], pre_ref[at, unit:]
+            sigma = jax.nn.sigmoid(pre_gate)
+            act = pre_gate * sigma
+            product = jnp.where(gate > 0.0, act * pre_up * back, 0.0)
+            gate_part = jnp.sum(product, axis=1, keepdims=True)
+            back = gate * back
+            d_ref[at, unit:] = (back * act).astype(jnp.bfloat16)
+            d_ref[at, :unit] = (back * pre_up * sigma * (1.0 + pre_gate * (1.0 - sigma))).astype(
+                jnp.bfloat16
+            )
+            out_ref[at, :features] = lax.dot_general(
+                d_ref[at, :],
+                win_ref[...],
+                (((1,), (1,)), ((), ())),
+                preferred_element_type=jnp.float32,
+            ).astype(out_dtype)
+            high = gate_part.astype(jnp.bfloat16).astype(jnp.float32)
+            rest = gate_part - high
+            middle = rest.astype(jnp.bfloat16).astype(jnp.float32)
+            lanes = lax.broadcasted_iota(jnp.int32, (gate_part.shape[0], back_width), 1)
+            side = jnp.zeros(lanes.shape, jnp.float32)
+            for i, piece in enumerate((high, middle, rest - middle)):
+                side = jnp.where(lanes == (i * halves + half) * experts + me, piece, side)
+            out_ref[at, features:] = side.astype(out_dtype)
+
+        blocks_of(rows, min(rows, 256), work)
+
+    shapes = (
+        jax.ShapeDtypeStruct((rows, width), jnp.bfloat16),
+        jax.ShapeDtypeStruct((rows, features + back_width), out_dtype),
+    )
+    operands = (where, cot, rows_in, pre, w_in, w_down)
+    return whole(kernel, shapes, operands, 1, 3 * rows * features * width)
+
+
+def pieces(x):
+    high = lax.reduce_precision(x, 8, 7)
+    rest = x - high
+    middle = lax.reduce_precision(rest, 8, 7)
+    return [high, middle, rest - middle]
+
+
+def dense_body(tokens, routes, gates, cotangent, w_gate, w_up, w_down):
+    token_count, features = tokens.shape
+    senders = lax.axis_size("expert")
+    halves = lax.axis_size("half")
+    experts = w_gate.shape[0] * senders
+    me = lax.axis_index("expert")
+    half = lax.axis_index("half")
+    rows = token_count // halves
+    bf16, f32 = jnp.bfloat16, jnp.float32
+
+    def padded(x):
+        return jnp.pad(x, ((0, 0), (0, -x.shape[1] % 128)))
+
+    def mine(x):
+        return lax.dynamic_slice_in_dim(x, half * rows, rows, 0)
+
+    onehot = routes[:, :, None] == jnp.arange(experts, dtype=jnp.int32)[None, None, :]
+    by_expert = jnp.sum(jnp.where(onehot, gates[:, :, None], 0.0), axis=1)
+    side = padded(jnp.concatenate(pieces(by_expert), axis=1)).astype(bf16)
+    where = jnp.stack([me, half]).astype(jnp.int32)
+    w_in = jnp.concatenate([w_gate[0], w_up[0]], axis=1)
+    w_out = w_down[0]
+
+    lower = half == 0
+    block = mine(jnp.concatenate([tokens, side], axis=1))
+    block, lower, where = lax.optimization_barrier((block, lower, where))
+    tok_one, tok_two = spread(block, senders)
+    cot_one, cot_two = spread(mine(cotangent), senders)
+    sums, saved = {}, {}
+    for tag, placed in (("f", tok_one), ("s", tok_two)):
+        rows_mine = assemble(placed)
+        rows_other = swap_half(rows_mine)
+        pre, weighted, out_mine = forward(rows_mine, w_in, w_out, where, experts, f32)
+        pre_o, weighted_o, out_other = forward(rows_other, w_in, w_out, where, experts, bf16)
+        sums[tag] = out_mine + wide(swap_half(out_other))
+        saved[tag] = [(rows_mine, pre, weighted), (rows_other, pre_o, weighted_o)]
+
+    all_rows, all_d, all_weighted, all_cots = [], [], [], []
+    slot_sums = {}
+    for tag, placed in (("f", cot_one), ("s", cot_two)):
+        cot_mine = assemble(placed)
+        cot_other = swap_half(cot_mine)
+        slots = []
+        for cot, kept, dtype in ((cot_mine, saved[tag][0], f32), (cot_other, saved[tag][1], bf16)):
+            rows_in, pre, weighted = kept
+            d, slot = backward(
+                cot, rows_in, pre, w_in, w_out, where, experts, halves, dtype
+            )
+            slots.append(slot)
+            all_rows.append(rows_in)
+            all_d.append(d)
+            all_weighted.append(weighted)
+            all_cots.append(cot)
+        slot_other = swap_half(slots[1])
+        slot_sums[tag] = slots[0] + wide(slot_other)
+
+    mix_kept, mix_shifted = collect_outputs(sums["f"], sums["s"], senders, slot_other)
+    grad_home, grad_shifted, mark = collect_gradients(slot_sums["f"], slot_sums["s"], senders)
+    mixed = finish_outputs(mix_kept, mix_shifted, senders, mark)
+    (grad_down,) = product_over_rows(all_weighted, all_cots)
+    grad_gate, grad_up = product_over_rows(all_rows, all_d, features)
+
+    def both(x, other):
+        return jnp.where(lower, stack(x, other), stack(other, x))
+
+    mixed = both(mixed, swap_half(mixed))
+    for moved in grad_shifted:
+        grad_home = grad_home + wide(after(moved, mixed))
+    grad_home = narrow(grad_home)
+    grad_other = swap_half(grad_home)
+    token_grad = both(grad_home[:, :features], grad_other[:, :features])
+    by_expert = both(grad_home[:, features:], grad_other[:, features:]).astype(f32)
+    by_expert = by_expert[:, : 3 * halves * experts].reshape(token_count, 3 * halves, experts)
+    by_expert = jnp.sum(by_expert, axis=1)
+    gate_grad = jnp.sum(jnp.where(onehot, by_expert[:, None, :], 0.0), axis=2)
+    return (mixed, token_grad, gate_grad, grad_gate, grad_up, grad_down)
+
+
+def body(tokens, routes, gates, cotangent, w_gate, w_up, w_down):
+    token_count, top_k = routes.shape
+    senders = lax.axis_size("expert")
+    halves = lax.axis_size("half")
+    capacity = 2 * token_count * top_k // (w_gate.shape[0] * senders)
+    dense = capacity >= token_count and w_gate.shape[0] == 1
+    if dense and halves == 2 and senders % 4 == 0 and token_count % 32 == 0:
+        return dense_body(tokens, routes, gates, cotangent, w_gate, w_up, w_down)
+    return slot_body(tokens, routes, gates, cotangent, w_gate, w_up, w_down)
+
+
 def solution(mesh):
     placed = (
         P("expert", None),

time: 337 us -> 183 us (0.54)
  blocking collectives: 166 us -> 0 us
  starting transfers between devices: 8.96 us -> 53.8 us
  matrix products: 42.6 us -> 0 us
  waiting for transfers between devices: 43 us -> 84.3 us
  local copies, waits for them, and re-layouts: 41 us -> 3.83 us
  Pallas kernels: 0 us -> 32.7 us
  other arithmetic: 20.4 us -> 6.84 us
  between operations: 14.3 us -> 1.33 us
    all_to_all x3 -> x0, blocking collectives: 166 us -> none  [the longest x1 58.1 us: body(): lax.all_to_all(scaled_part, 'expert', split_axis=0, concat_axis=0, tiled=...]
    ppermute x0 -> x50, waiting for transfers between devices: none -> 84.3 us  [the longest x28 60.6 us: flip(): return lax.ppermute(x, 'expert', flipped(n, bit))]
    ppermute x0 -> x50, starting transfers between devices: none -> 53.8 us  [the longest x28 31 us: flip(): return lax.ppermute(x, 'expert', flipped(n, bit))]
    dot_general x9 -> x0, matrix products: 42.6 us -> none  [the longest x6 27.3 us: contract(): lax.dot_general(left, right, (((left_dim,), (right_dim,)), ((), ())), pre...]
    gather x5 -> x0, local copies, waits for them, and re-layouts: 35.1 us -> none  [the longest x1 8.25 us: body(): out_home.reshape(experts * capacity, features)[target]]
    pallas_call x0 -> x14, Pallas kernels: none -> 32.7 us  [the longest x12 20.4 us: whole(): pl.pallas_call(kernel, out_shape=out_shapes, in_specs=[SMEM] * scalars +...]
    all_to_all x1 -> x0, waiting for transfers between devices: 29.9 us -> none  [body(): lax.all_to_all(rows_part, 'expert', split_axis=0, concat_axis=0, tiled=True)]
    reduce_scatter x2 -> x0, waiting for transfers between devices: 10.9 us -> none  [the longest x1 10.8 us: body(): lax.psum_scatter(grad_part, 'half', scatter_dimension=1, tiled=True)]
  transfers between devices with their start and end apart: 7 -> 50, of which waited for: 3 -> 14; matrix products, arithmetic and copies ran while one was open for 18% -> 4% of each run, Pallas kernels for 0% -> 18%
where the time goes in v1:
time: 183 us
  waiting for transfers between devices  84.3 us (46%)
  starting transfers between devices  53.8 us (29%)
  Pallas kernels  32.7 us (18%)
  other arithmetic  6.84 us (4%)
  local copies, waits for them, and re-layouts  3.83 us (2%)
    ppermute x28, waiting for transfers between devices, flip(): return lax.ppermute(x, 'expert', flipped(n, bit))  60.6 us
    ppermute x28, starting transfers between devices, flip(): return lax.ppermute(x, 'expert', flipped(n, bit))  31 us
    ppermute x6, waiting for transfers between devices, shift_home(): lax.ppermute(narrow(block), 'expert', [(d, s) for s, d in rolled(n, j)])  23.6 us
    pallas_call x12, Pallas kernels, whole(): pl.pallas_call(kernel, out_shape=out_shapes, in_specs=[SMEM] * scalars +...  20.4 us
    pallas_call x2, Pallas kernels, product_over_rows(): pl.pallas_call(kernel, grid=(features // tile,), out_shape=out_shape, in_...  12.3 us
    ppermute x6, starting transfers between devices, spread(): lax.ppermute(block, 'expert', rolled(n, j))  12.2 us
    ppermute x6, starting transfers between devices, shift_home(): lax.ppermute(narrow(block), 'expert', [(d, s) for s, d in rolled(n, j)])  8.57 us
  transfers between devices with their start and end apart: 50, of which 14 were waited for; matrix products, arithmetic and copies ran while one was open for 4% of the time, Pallas kernels for 18%

profile of v1, /device:TPU:0, one launch (start us, length us, event | category | flops | bytes accessed | tf_op | source)
XLA Modules:
  0.0 182.8 jit_solution(10140732149765863139)
XLA Ops:
  1.6 3.1 %collective-permute-start.19 = (bf16[32,2048]{1,0:T(8,128)(2,1)S(1)}, bf16[32,2048]{1,0:T(8,128)(2,1)S(1)}, u32[]{:S(2)}, u32[]{:S(2)}) collective-permute-start(bf16[32,2048]{1,0:T(8,128)(2,1)S(1)} %constant_dynamic-slice_fusion.1), channel_id=1, source_target_pairs={{24,0},{26,2},{28,4},{30,6},{0,8},{2,10},{4,12},{6,14},{8,16},{10,... | collective-permute-start | bytes 393224 | tf_op jit(solution)/shard_map/ppermute | solution.py:136
  4.7 2.1 %collective-permute-start.18 = (bf16[32,2048]{1,0:T(8,128)(2,1)S(1)}, bf16[32,2048]{1,0:T(8,128)(2,1)S(1)}, u32[]{:S(2)}, u32[]{:S(2)}) collective-permute-start(bf16[32,2048]{1,0:T(8,128)(2,1)S(1)} %constant_dynamic-slice_fusion.1), channel_id=1, source_target_pairs={{8,0},{10,2},{12,4},{14,6},{16,8},{18,10},{20,12},{22,14},{24,16},... | collective-permute-start | bytes 393224 | tf_op jit(solution)/shard_map/ppermute | solution.py:136
  8.6 1.6 collective-permute-start.23
  12.2 2.2 %collective-permute-start.2 = (bf16[32,2176]{1,0:T(8,128)(2,1)S(1)}, bf16[32,2176]{1,0:T(8,128)(2,1)S(1)}, u32[]{:S(2)}, u32[]{:S(2)}) collective-permute-start(bf16[32,2176]{1,0:T(8,128)(2,1)S(1)} %fusion.7), channel_id=1, source_target_pairs={{16,0},{18,2},{20,4},{22,6},{24,8},{26,10},{28,12},{30,14},{0,16},... | collective-permute-start | bytes 417800 | tf_op jit(solution)/shard_map/ppermute | solution.py:136
  14.4 1.6 collective-permute-start.3
  16.0 2.8 %collective-permute-done.3.refs_2_ = bf16[16,2176]{1,0:T(8,128)(2,1)S(1)} collective-permute-done((bf16[16,2176]{1,0:T(8,128)(2,1)S(1)}, bf16[16,2176]{1,0:T(8,128)(2,1)S(1)}, u32[]{:S(2)}, u32[]{:S(2)}) %collective-permute-start.3) | collective-permute-done | bytes 69664 | tf_op jit(solution)/shard_map/ppermute | solution.py:125
  19.1 3.9 %collective-permute-done.5.refs_6_ = bf16[16,2176]{1,0:T(8,128)(2,1)S(1)} collective-permute-done((bf16[16,2176]{1,0:T(8,128)(2,1)S(1)}, bf16[16,2176]{1,0:T(8,128)(2,1)S(1)}, u32[]{:S(2)}, u32[]{:S(2)}) %collective-permute-start.5) | collective-permute-done | bytes 69664 | tf_op jit(solution)/shard_map/ppermute | solution.py:125
  23.1 3.9 %collective-permute-start = (bf16[32,2176]{1,0:T(8,128)(2,1)S(1)}, bf16[32,2176]{1,0:T(8,128)(2,1)S(1)}, u32[]{:S(2)}, u32[]{:S(2)}) collective-permute-start(bf16[32,2176]{1,0:T(8,128)(2,1)S(1)} %fusion.7), channel_id=1, source_target_pairs={{8,0},{10,2},{12,4},{14,6},{16,8},{18,10},{20,12},{22,14},{24,16},... | collective-permute-start | bytes 417800 | tf_op jit(solution)/shard_map/ppermute | solution.py:136
  27.0 1.6 collective-permute-start.16
  29.3 1.6 collective-permute-start.11
  32.2 1.6 collective-permute-start.9
  33.8 5.7 %collective-permute-done.21.refs_3_ = bf16[48,2048]{1,0:T(8,128)(2,1)S(1)} collective-permute-done((bf16[48,2048]{1,0:T(8,128)(2,1)S(1)}, bf16[48,2048]{1,0:T(8,128)(2,1)S(1)}, u32[]{:S(2)}, u32[]{:S(2)}) %collective-permute-start.21) | collective-permute-done | bytes 196640 | tf_op jit(solution)/shard_map/ppermute | solution.py:125
  39.5 1.3 collective-permute-start.4
  41.5 5.2 %collective-permute-done.6.refs_7_ = bf16[48,2176]{1,0:T(8,128)(2,1)S(1)} collective-permute-done((bf16[48,2176]{1,0:T(8,128)(2,1)S(1)}, bf16[48,2176]{1,0:T(8,128)(2,1)S(1)}, u32[]{:S(2)}, u32[]{:S(2)}) %collective-permute-start.6) | collective-permute-done | bytes 208928 | tf_op jit(solution)/shard_map/ppermute | solution.py:125
  48.3 1.4 collective-permute-start.26
  49.7 1.5 collective-permute-start.22
  51.2 7.2 %collective-permute-done.12.refs_3_ = bf16[96,2176]{1,0:T(8,128)(2,1)S(1)} collective-permute-done((bf16[96,2176]{1,0:T(8,128)(2,1)S(1)}, bf16[96,2176]{1,0:T(8,128)(2,1)S(1)}, u32[]{:S(2)}, u32[]{:S(2)}) %collective-permute-start.12) | collective-permute-done | bytes 417824 | tf_op jit(solution)/shard_map/ppermute | solution.py:125
  58.5 1.8 collective-permute-done.10.refs_1_
  60.8 10.2 %collective-permute-done.17.refs_0_ = bf16[32,2048]{1,0:T(8,128)(2,1)S(1)} collective-permute-done((bf16[32,2048]{1,0:T(8,128)(2,1)S(1)}, bf16[32,2048]{1,0:T(8,128)(2,1)S(1)}, u32[]{:S(2)}, u32[]{:S(2)}) %collective-permute-start.17) | collective-permute-done | bytes 131104 | tf_op jit(solution)/shard_map/ppermute | solution.py:125
  71.9 1.1 copy-done
  73.1 2.7 %shard_map.120 = (f32[256,768]{1,0:T(8,128)S(1)}, bf16[256,384]{1,0:T(8,128)(2,1)S(1)}, bf16[256,2048]{1,0:T(8,128)(2,1)S(1)}) custom-call(s32[2]{0:T(128)S(1)} %pad_add_fusion.where_ref, bf16[256,2176]{1,0:T(8,128)(2,1)S(1)} %collective-permute-done.7.x_ref.side_ref.refs_1_, bf16[2048,768]{1,0:T(8,128)(2,1)S(1)} %pad_maximum_fusion.win_ref, ...), custom_call_target="tpu_custom_call" | custom-call | flops 1207959552 | bytes 7864328 | tf_op jit(solution)/shard_map/pallas_call | solution.py:246
  75.9 2.7 %shard_map.119 = (f32[256,768]{1,0:T(8,128)S(1)}, bf16[256,384]{1,0:T(8,128)(2,1)S(1)}, f32[256,2048]{1,0:T(8,128)S(1)}) custom-call(s32[2]{0:T(128)S(1)} %pad_add_fusion.where_ref, bf16[256,2176]{1,0:T(8,128)(2,1)S(1)} %shard_map.118.x_ref.side_ref.refs_0_, bf16[2048,768]{1,0:T(8,128)(2,1)S(1)} %pad_maximum_fusion.win_ref, bf16[384,2048]{1,0:T(8,128)(2,1)S(1)} %bitcast.7), custom_call_target="tpu_custom_call" | custom-call | flops 1207959552 | bytes 8912904 | tf_op jit(solution)/shard_map/pallas_call | solution.py:246
  78.6 2.3 %shard_map.127 = (bf16[256,768]{1,0:T(8,128)(2,1)S(1)}, f32[256,2176]{1,0:T(8,128)S(1)}) custom-call(s32[2]{0:T(128)S(1)} %pad_add_fusion.where_ref, bf16[256,2048]{1,0:T(8,128)(2,1)S(1)} %shard_map.126.cot_ref.refs_4_, bf16[256,2176]{1,0:T(8,128)(2,1)S(1)} %shard_map.118.x_ref.side_ref.refs_0_, f32[256,768]{1,0:T(8,128)S(1)} %get-tuple-element.50.pre_ref, ...), custom_call_target="tpu_custom_call" | custom-call | flops 1207959552 | bytes 10289160 | tf_op jit(solution)/shard_map/pallas_call | solution.py:246
  80.9 2.7 %shard_map.122 = (f32[256,768]{1,0:T(8,128)S(1)}, bf16[256,384]{1,0:T(8,128)(2,1)S(1)}, f32[256,2048]{1,0:T(8,128)S(1)}) custom-call(s32[2]{0:T(128)S(1)} %pad_add_fusion.where_ref, bf16[256,2176]{1,0:T(8,128)(2,1)S(1)} %shard_map.121.x_ref.side_ref.refs_2_, bf16[2048,768]{1,0:T(8,128)(2,1)S(1)} %pad_maximum_fusion.win_ref, bf16[384,2048]{1,0:T(8,128)(2,1)S(1)} %bitcast.9), custom_call_target="tpu_custom_call" | custom-call | flops 1207959552 | bytes 8912904 | tf_op jit(solution)/shard_map/pallas_call | solution.py:246
  83.6 2.3 %shard_map.128 = (bf16[256,768]{1,0:T(8,128)(2,1)S(1)}, bf16[256,2176]{1,0:T(8,128)(2,1)S(1)}) custom-call(s32[2]{0:T(128)S(1)} %pad_add_fusion.where_ref, bf16[256,2048]{1,0:T(8,128)(2,1)S(1)} %collective-permute-done.31.cot_ref.refs_5_, bf16[256,2176]{1,0:T(8,128)(2,1)S(1)} %collective-permute-done.7.x_ref.side_ref.refs_1_, ...), custom_call_target="tpu_custom_call" | custom-call | flops 1207959552 | bytes 9175048 | tf_op jit(solution)/shard_map/pallas_call | solution.py:246
  86.5 2.3 %shard_map.129 = (bf16[256,768]{1,0:T(8,128)(2,1)S(1)}, f32[256,2176]{1,0:T(8,128)S(1)}) custom-call(s32[2]{0:T(128)S(1)} %pad_add_fusion.where_ref, bf16[256,2048]{1,0:T(8,128)(2,1)S(1)} %shard_map.124.cot_ref.refs_6_, bf16[256,2176]{1,0:T(8,128)(2,1)S(1)} %shard_map.121.x_ref.side_ref.refs_2_, f32[256,768]{1,0:T(8,128)S(1)} %get-tuple-element.54.pre_ref, ...), custom_call_target="tpu_custom_call" | custom-call | flops 1207959552 | bytes 10289160 | tf_op jit(solution)/shard_map/pallas_call | solution.py:246
  88.8 2.9 %shard_map.123 = (f32[256,768]{1,0:T(8,128)S(1)}, bf16[256,384]{1,0:T(8,128)(2,1)S(1)}, bf16[256,2048]{1,0:T(8,128)(2,1)S(1)}) custom-call(s32[2]{0:T(128)S(1)} %pad_add_fusion.where_ref, bf16[256,2176]{1,0:T(8,128)(2,1)S(1)} %collective-permute-done.13.x_ref.side_ref.refs_3_, bf16[2048,768]{1,0:T(8,128)(2,1)S(1)} %pad_maximum_fusion.win_ref, ...), custom_call_target="tpu_custom_call" | custom-call | flops 1207959552 | bytes 7864328 | tf_op jit(solution)/shard_map/pallas_call | solution.py:246
  91.7 2.3 %shard_map.125 = (bf16[256,768]{1,0:T(8,128)(2,1)S(1)}, bf16[256,2176]{1,0:T(8,128)(2,1)S(1)}) custom-call(s32[2]{0:T(128)S(1)} %pad_add_fusion.where_ref, bf16[256,2048]{1,0:T(8,128)(2,1)S(1)} %collective-permute-done.27.cot_ref.refs_7_, bf16[256,2176]{1,0:T(8,128)(2,1)S(1)} %collective-permute-done.13.x_ref.side_ref.refs_3_, ...), custom_call_target="tpu_custom_call" | custom-call | flops 1207959552 | bytes 9175048 | tf_op jit(solution)/shard_map/pallas_call | solution.py:246
  94.6 7.0 %shard_map.130 = (bf16[1,2048,384]{2,1,0:T(8,128)(2,1)}, bf16[1,2048,384]{2,1,0:T(8,128)(2,1)}) custom-call(bf16[256,2176]{1,0:T(8,128)(2,1)S(1)} %shard_map.118.x_ref.side_ref.refs_0_, bf16[256,2176]{1,0:T(8,128)(2,1)S(1)} %collective-permute-done.7.x_ref.side_ref.refs_1_, bf16[256,2176]{1,0:T(8,128)(2,1)S(1)} %shard_map.121.x_ref.side_ref.refs_2_, ...), custom_call_target="tpu_custom_call" | custom-call | flops 3221225472 | tf_op jit(solution)/shard_map/pallas_call | solution.py:306
  103.4 1.3 collective-permute-start.29
  105.8 1.6 collective-permute-start.40
  107.5 1.4 collective-permute-start.44
  108.9 10.9 %collective-permute-done.40 = bf16[32,2176]{1,0:T(8,128)(2,1)S(1)} collective-permute-done((bf16[32,2176]{1,0:T(8,128)(2,1)S(1)}, bf16[32,2176]{1,0:T(8,128)(2,1)S(1)}, u32[]{:S(2)}, u32[]{:S(2)}) %collective-permute-start.40) | collective-permute-done | bytes 139296 | tf_op jit(solution)/shard_map/ppermute | solution.py:125
  121.2 1.3 collective-permute-start.41
  122.6 7.9 %collective-permute-done.41 = bf16[16,2176]{1,0:T(8,128)(2,1)S(1)} collective-permute-done((bf16[16,2176]{1,0:T(8,128)(2,1)S(1)}, bf16[16,2176]{1,0:T(8,128)(2,1)S(1)}, u32[]{:S(2)}, u32[]{:S(2)}) %collective-permute-start.41) | collective-permute-done | bytes 69664 | tf_op jit(solution)/shard_map/ppermute | solution.py:125
  130.4 1.5 collective-permute-start.34
  132.0 2.8 %collective-permute-done.34 = bf16[16,2176]{1,0:T(8,128)(2,1)S(1)} collective-permute-done((bf16[16,2176]{1,0:T(8,128)(2,1)S(1)}, bf16[16,2176]{1,0:T(8,128)(2,1)S(1)}, u32[]{:S(2)}, u32[]{:S(2)}) %collective-permute-start.34) | collective-permute-done | bytes 69664 | tf_op jit(solution)/shard_map/ppermute | solution.py:125
  134.9 1.4 collective-permute-start.43
  136.4 1.6 collective-permute-start.45
  138.8 2.1 %collective-permute-start.30 = (bf16[64,2048]{1,0:T(8,128)(2,1)S(1)}, bf16[64,2048]{1,0:T(8,128)(2,1)S(1)}, u32[]{:S(2)}, u32[]{:S(2)}) collective-permute-start(bf16[64,2048]{1,0:T(8,128)(2,1)S(1)} %pad_maximum_fusion.7), channel_id=1, source_target_pairs={{0,8},{2,10},{4,12},{6,14},{8,16},{10,18},{12,20},{14,22},{16,24},... | collective-permute-start | bytes 786440 | tf_op jit(solution)/shard_map/ppermute | solution.py:170
  140.9 1.3 collective-permute-done.45
  142.4 1.1 collective-permute-start.47
  143.5 17.1 %collective-permute-done.36 = bf16[64,2048]{1,0:T(8,128)(2,1)S(1)} collective-permute-done((bf16[64,2048]{1,0:T(8,128)(2,1)S(1)}, bf16[64,2048]{1,0:T(8,128)(2,1)S(1)}, u32[]{:S(2)}, u32[]{:S(2)}) %collective-permute-start.36) | collective-permute-done | bytes 262176 | tf_op jit(solution)/shard_map/ppermute | solution.py:170
  161.6 1.5 collective-permute-start.38
  163.1 3.4 %collective-permute-start.48 = (bf16[32,2176]{1,0:T(8,128)(2,1)S(1)}, bf16[32,2176]{1,0:T(8,128)(2,1)S(1)}, u32[]{:S(2)}, u32[]{:S(2)}) collective-permute-start(bf16[32,2176]{1,0:T(8,128)(2,1)S(1)} %pad_maximum_fusion.20), channel_id=1, source_target_pairs={{0,16},{2,18},{4,20},{6,22},{8,24},{10,26},{12,28},{14,30},{16,0},... | collective-permute-start | bytes 417800 | tf_op jit(solution)/shard_map/ppermute | solution.py:170
  166.7 1.8 collective-permute-start.46
  169.3 6.5 %collective-permute-done.48 = bf16[32,2176]{1,0:T(8,128)(2,1)S(1)} collective-permute-done((bf16[32,2176]{1,0:T(8,128)(2,1)S(1)}, bf16[32,2176]{1,0:T(8,128)(2,1)S(1)}, u32[]{:S(2)}, u32[]{:S(2)}) %collective-permute-start.48) | collective-permute-done | bytes 139296 | tf_op jit(solution)/shard_map/ppermute | solution.py:170
  176.0 5.3 %shard_map.131 = bf16[1,384,2048]{2,1,0:T(8,128)(2,1)} custom-call(bf16[256,384]{1,0:T(8,128)(2,1)S(1)} %get-tuple-element.68.refs_0_, bf16[256,384]{1,0:T(8,128)(2,1)S(1)} %get-tuple-element.69.refs_1_, bf16[256,384]{1,0:T(8,128)(2,1)S(1)} %get-tuple-element.70.refs_2_, bf16[256,384]{1,0:T(8,128)(2,1)S(1)} %get-tuple-element.71.refs_3_, ...), custom_call_target="tpu_custom_call" | custom-call | flops 1610612736 | tf_op jit(solution)/shard_map/pallas_call | solution.py:306
  (155 shorter events, 21.2 us)
Async XLA Ops:
  1.6 21.6 %collective-permute-start.19 = (bf16[32,2048]{1,0:T(8,128)(2,1)S(1)}, bf16[32,2048]{1,0:T(8,128)(2,1)S(1)}, u32[]{:S(2)}, u32[]{:S(2)}) collective-permute-start(bf16[32,2048]{1,0:T(8,128)(2,1)S(1)} %constant_dynamic-slice_fusion.1), channel_id=1, source_target_pairs={{24,0},{26,2},{28,4},{30,6},{0,8},{2,10},{4,12},{6,14},{8,16},{10,... | collective-permute-start | bytes 393224 | tf_op jit(solution)/shard_map/ppermute | solution.py:136
  4.7 22.3 %collective-permute-start.18 = (bf16[32,2048]{1,0:T(8,128)(2,1)S(1)}, bf16[32,2048]{1,0:T(8,128)(2,1)S(1)}, u32[]{:S(2)}, u32[]{:S(2)}) collective-permute-start(bf16[32,2048]{1,0:T(8,128)(2,1)S(1)} %constant_dynamic-slice_fusion.1), channel_id=1, source_target_pairs={{8,0},{10,2},{12,4},{14,6},{16,8},{18,10},{20,12},{22,14},{24,16},... | collective-permute-start | bytes 393224 | tf_op jit(solution)/shard_map/ppermute | solution.py:136
  6.8 21.8 %collective-permute-start.20 = (bf16[32,2048]{1,0:T(8,128)(2,1)S(1)}, bf16[32,2048]{1,0:T(8,128)(2,1)S(1)}, u32[]{:S(2)}, u32[]{:S(2)}) collective-permute-start(bf16[32,2048]{1,0:T(8,128)(2,1)S(1)} %constant_dynamic-slice_fusion.1), channel_id=1, source_target_pairs={{16,0},{18,2},{20,4},{22,6},{24,8},{26,10},{28,12},{30,14},{0,16},... | collective-permute-start | bytes 393224 | tf_op jit(solution)/shard_map/ppermute | solution.py:136
  8.6 5.8 %collective-permute-start.23 = (bf16[16,2048]{1,0:T(8,128)(2,1)S(1)}, bf16[16,2048]{1,0:T(8,128)(2,1)S(1)}, u32[]{:S(2)}, u32[]{:S(2)}) collective-permute-start(bf16[16,2048]{1,0:T(8,128)(2,1)S(1)} %get-tuple-element.118.refs_4_), channel_id=1, source_target_pairs={{0,4},{2,6},{4,0},{6,2},{8,12},{10,14},{12,8},{14,10},{16,20},{18,... | collective-permute-start | bytes 196616 | tf_op jit(solution)/shard_map/ppermute | solution.py:125
  12.2 17.1 %collective-permute-start.2 = (bf16[32,2176]{1,0:T(8,128)(2,1)S(1)}, bf16[32,2176]{1,0:T(8,128)(2,1)S(1)}, u32[]{:S(2)}, u32[]{:S(2)}) collective-permute-start(bf16[32,2176]{1,0:T(8,128)(2,1)S(1)} %fusion.7), channel_id=1, source_target_pairs={{16,0},{18,2},{20,4},{22,6},{24,8},{26,10},{28,12},{30,14},{0,16},... | collective-permute-start | bytes 417800 | tf_op jit(solution)/shard_map/ppermute | solution.py:136
  14.4 4.4 %collective-permute-start.3 = (bf16[16,2176]{1,0:T(8,128)(2,1)S(1)}, bf16[16,2176]{1,0:T(8,128)(2,1)S(1)}, u32[]{:S(2)}, u32[]{:S(2)}) collective-permute-start(bf16[16,2176]{1,0:T(8,128)(2,1)S(1)} %get-tuple-element.133.refs_0_), channel_id=1, source_target_pairs={{0,2},{2,0},{4,6},{6,4},{8,10},{10,8},{12,14},{14,12},{16,18},{18,... | collective-permute-start | bytes 208904 | tf_op jit(solution)/shard_map/ppermute | solution.py:125
  18.8 4.3 %collective-permute-start.5 = (bf16[16,2176]{1,0:T(8,128)(2,1)S(1)}, bf16[16,2176]{1,0:T(8,128)(2,1)S(1)}, u32[]{:S(2)}, u32[]{:S(2)}) collective-permute-start(bf16[16,2176]{1,0:T(8,128)(2,1)S(1)} %get-tuple-element.132.refs_4_), channel_id=1, source_target_pairs={{0,4},{2,6},{4,0},{6,2},{8,12},{10,14},{12,8},{14,10},{16,20},{18,... | collective-permute-start | bytes 208904 | tf_op jit(solution)/shard_map/ppermute | solution.py:125
  23.1 7.7 %collective-permute-start.1 = (bf16[32,2176]{1,0:T(8,128)(2,1)S(1)}, bf16[32,2176]{1,0:T(8,128)(2,1)S(1)}, u32[]{:S(2)}, u32[]{:S(2)}) collective-permute-start(bf16[32,2176]{1,0:T(8,128)(2,1)S(1)} %fusion.7), channel_id=1, source_target_pairs={{24,0},{26,2},{28,4},{30,6},{0,8},{2,10},{4,12},{6,14},{8,16},{10,... | collective-permute-start | bytes 417800 | tf_op jit(solution)/shard_map/ppermute | solution.py:136
  23.1 8.4 %collective-permute-start = (bf16[32,2176]{1,0:T(8,128)(2,1)S(1)}, bf16[32,2176]{1,0:T(8,128)(2,1)S(1)}, u32[]{:S(2)}, u32[]{:S(2)}) collective-permute-start(bf16[32,2176]{1,0:T(8,128)(2,1)S(1)} %fusion.7), channel_id=1, source_target_pairs={{8,0},{10,2},{12,4},{14,6},{16,8},{18,10},{20,12},{22,14},{24,16},... | collective-permute-start | bytes 417800 | tf_op jit(solution)/shard_map/ppermute | solution.py:136
  27.0 5.2 %collective-permute-start.16 = (bf16[16,2048]{1,0:T(8,128)(2,1)S(1)}, bf16[16,2048]{1,0:T(8,128)(2,1)S(1)}, u32[]{:S(2)}, u32[]{:S(2)}) collective-permute-start(bf16[16,2048]{1,0:T(8,128)(2,1)S(1)} %get-tuple-element.119.refs_0_), channel_id=1, source_target_pairs={{0,2},{2,0},{4,6},{6,4},{8,10},{10,8},{12,14},{14,12},{16,18},{18,... | collective-permute-start | bytes 196616 | tf_op jit(solution)/shard_map/ppermute | solution.py:125
  28.6 19.1 %collective-permute-start.24 = (bf16[32,2048]{1,0:T(8,128)(2,1)S(1)}, bf16[32,2048]{1,0:T(8,128)(2,1)S(1)}, u32[]{:S(2)}, u32[]{:S(2)}) collective-permute-start(bf16[32,2048]{1,0:T(8,128)(2,1)S(1)} %pad_maximum_fusion.22), channel_id=1, source_target_pairs={{0,2},{2,0},{4,6},{6,4},{8,10},{10,8},{12,14},{14,12},{16,18},{18,... | collective-permute-start | bytes 393224 | tf_op jit(solution)/shard_map/ppermute | solution.py:125
  29.3 19.0 %collective-permute-start.11 = (bf16[32,2176]{1,0:T(8,128)(2,1)S(1)}, bf16[32,2176]{1,0:T(8,128)(2,1)S(1)}, u32[]{:S(2)}, u32[]{:S(2)}) collective-permute-start(bf16[32,2176]{1,0:T(8,128)(2,1)S(1)} %pad_maximum_fusion.15), channel_id=1, source_target_pairs={{0,2},{2,0},{4,6},{6,4},{8,10},{10,8},{12,14},{14,12},{16,18},{18,... | collective-permute-start | bytes 417800 | tf_op jit(solution)/shard_map/ppermute | solution.py:125
  30.8 8.7 %collective-permute-start.21 = (bf16[48,2048]{1,0:T(8,128)(2,1)S(1)}, bf16[48,2048]{1,0:T(8,128)(2,1)S(1)}, u32[]{:S(2)}, u32[]{:S(2)}) collective-permute-start(bf16[48,2048]{1,0:T(8,128)(2,1)S(1)} %pad_maximum_fusion.12.refs_1_), channel_id=1, source_target_pairs={{0,2},{2,0},{4,6},{6,4},{8,10},{10,8},{12,14},{14,12},{16,18},{18,... | collective-permute-start | bytes 589832 | tf_op jit(solution)/shard_map/ppermute | solution.py:125
  31.6 9.3 %collective-permute-start.25 = (bf16[48,2048]{1,0:T(8,128)(2,1)S(1)}, bf16[48,2048]{1,0:T(8,128)(2,1)S(1)}, u32[]{:S(2)}, u32[]{:S(2)}) collective-permute-start(bf16[48,2048]{1,0:T(8,128)(2,1)S(1)} %pad_maximum_fusion.13.refs_5_), channel_id=1, source_target_pairs={{0,4},{2,6},{4,0},{6,2},{8,12},{10,14},{12,8},{14,10},{16,20},{18,... | collective-permute-start | bytes 589832 | tf_op jit(solution)/shard_map/ppermute | solution.py:125
  32.2 17.5 %collective-permute-start.9 = (bf16[32,2176]{1,0:T(8,128)(2,1)S(1)}, bf16[32,2176]{1,0:T(8,128)(2,1)S(1)}, u32[]{:S(2)}, u32[]{:S(2)}) collective-permute-start(bf16[32,2176]{1,0:T(8,128)(2,1)S(1)} %pad_maximum_fusion.14), channel_id=1, source_target_pairs={{0,4},{2,6},{4,0},{6,2},{8,12},{10,14},{12,8},{14,10},{16,20},{18,... | collective-permute-start | bytes 417800 | tf_op jit(solution)/shard_map/ppermute | solution.py:125
  39.5 7.9 %collective-permute-start.4 = (bf16[48,2176]{1,0:T(8,128)(2,1)S(1)}, bf16[48,2176]{1,0:T(8,128)(2,1)S(1)}, u32[]{:S(2)}, u32[]{:S(2)}) collective-permute-start(bf16[48,2176]{1,0:T(8,128)(2,1)S(1)} %pad_maximum_fusion.10.refs_1_), channel_id=1, source_target_pairs={{0,2},{2,0},{4,6},{6,4},{8,10},{10,8},{12,14},{14,12},{16,18},{18,... | collective-permute-start | bytes 626696 | tf_op jit(solution)/shard_map/ppermute | solution.py:125
  40.8 5.8 %collective-permute-start.6 = (bf16[48,2176]{1,0:T(8,128)(2,1)S(1)}, bf16[48,2176]{1,0:T(8,128)(2,1)S(1)}, u32[]{:S(2)}, u32[]{:S(2)}) collective-permute-start(bf16[48,2176]{1,0:T(8,128)(2,1)S(1)} %pad_maximum_fusion.11.refs_5_), channel_id=1, source_target_pairs={{0,4},{2,6},{4,0},{6,2},{8,12},{10,14},{12,8},{14,10},{16,20},{18,... | collective-permute-start | bytes 626696 | tf_op jit(solution)/shard_map/ppermute | solution.py:125
  46.7 11.7 %collective-permute-start.12 = (bf16[96,2176]{1,0:T(8,128)(2,1)S(1)}, bf16[96,2176]{1,0:T(8,128)(2,1)S(1)}, u32[]{:S(2)}, u32[]{:S(2)}) collective-permute-start(bf16[96,2176]{1,0:T(8,128)(2,1)S(1)} %pad_maximum_fusion.2), channel_id=1, source_target_pairs={{0,2},{2,0},{4,6},{6,4},{8,10},{10,8},{12,14},{14,12},{16,18},{18,... | collective-permute-start | bytes 1253384 | tf_op jit(solution)/shard_map/ppermute | solution.py:125
  47.5 24.4 %collective-permute-start.7 = (bf16[256,2176]{1,0:T(8,128)(2,1)S(1)}, bf16[256,2176]{1,0:T(8,128)(2,1)S(1)}, u32[]{:S(2)}, u32[]{:S(2)}) collective-permute-start(bf16[256,2176]{1,0:T(8,128)(2,1)S(1)} %shard_map.118.x_ref.side_ref.refs_0_), channel_id=1, source_target_pairs={{0,1},{1,0},{2,3},{3,2},{4,5},{5,4},{6,7},{7,6},{8,9},{9,8},{10,11... | collective-permute-start | bytes 3342344 | tf_op jit(solution)/shard_map/ppermute | solution.py:110
  47.7 12.6 %collective-permute-start.10 = (bf16[96,2176]{1,0:T(8,128)(2,1)S(1)}, bf16[96,2176]{1,0:T(8,128)(2,1)S(1)}, u32[]{:S(2)}, u32[]{:S(2)}) collective-permute-start(bf16[96,2176]{1,0:T(8,128)(2,1)S(1)} %pad_maximum_fusion.1), channel_id=1, source_target_pairs={{0,4},{2,6},{4,0},{6,2},{8,12},{10,14},{12,8},{14,10},{16,20},{18,... | collective-permute-start | bytes 1253384 | tf_op jit(solution)/shard_map/ppermute | solution.py:125
  48.3 22.7 %collective-permute-start.26 = (bf16[96,2048]{1,0:T(8,128)(2,1)S(1)}, bf16[96,2048]{1,0:T(8,128)(2,1)S(1)}, u32[]{:S(2)}, u32[]{:S(2)}) collective-permute-start(bf16[96,2048]{1,0:T(8,128)(2,1)S(1)} %pad_maximum_fusion.6), channel_id=1, source_target_pairs={{0,2},{2,0},{4,6},{6,4},{8,10},{10,8},{12,14},{14,12},{16,18},{18,... | collective-permute-start | bytes 1179656 | tf_op jit(solution)/shard_map/ppermute | solution.py:125
  49.7 21.4 %collective-permute-start.22 = (bf16[96,2048]{1,0:T(8,128)(2,1)S(1)}, bf16[96,2048]{1,0:T(8,128)(2,1)S(1)}, u32[]{:S(2)}, u32[]{:S(2)}) collective-permute-start(bf16[96,2048]{1,0:T(8,128)(2,1)S(1)} %pad_maximum_fusion.5), channel_id=1, source_target_pairs={{0,4},{2,6},{4,0},{6,2},{8,12},{10,14},{12,8},{14,10},{16,20},{18,... | collective-permute-start | bytes 1179656 | tf_op jit(solution)/shard_map/ppermute | solution.py:125
  58.4 25.2 %collective-permute-start.31 = (bf16[256,2048]{1,0:T(8,128)(2,1)S(1)}, bf16[256,2048]{1,0:T(8,128)(2,1)S(1)}, u32[]{:S(2)}, u32[]{:S(2)}) collective-permute-start(bf16[256,2048]{1,0:T(8,128)(2,1)S(1)} %shard_map.126.cot_ref.refs_4_), channel_id=1, source_target_pairs={{0,1},{1,0},{2,3},{3,2},{4,5},{5,4},{6,7},{7,6},{8,9},{9,8},{10,11... | collective-permute-start | bytes 3145736 | tf_op jit(solution)/shard_map/ppermute | solution.py:110
  60.3 10.8 %collective-permute-start.17 = (bf16[32,2048]{1,0:T(8,128)(2,1)S(1)}, bf16[32,2048]{1,0:T(8,128)(2,1)S(1)}, u32[]{:S(2)}, u32[]{:S(2)}) collective-permute-start(bf16[32,2048]{1,0:T(8,128)(2,1)S(1)} %pad_maximum_fusion.21), channel_id=1, source_target_pairs={{0,4},{2,6},{4,0},{6,2},{8,12},{10,14},{12,8},{14,10},{16,20},{18,... | collective-permute-start | bytes 393224 | tf_op jit(solution)/shard_map/ppermute | solution.py:125
  71.0 17.7 %collective-permute-start.13 = (bf16[256,2176]{1,0:T(8,128)(2,1)S(1)}, bf16[256,2176]{1,0:T(8,128)(2,1)S(1)}, u32[]{:S(2)}, u32[]{:S(2)}) collective-permute-start(bf16[256,2176]{1,0:T(8,128)(2,1)S(1)} %shard_map.121.x_ref.side_ref.refs_2_), channel_id=1, source_target_pairs={{0,1},{1,0},{2,3},{3,2},{4,5},{5,4},{6,7},{7,6},{8,9},{9,8},{10,11... | collective-permute-start | bytes 3342344 | tf_op jit(solution)/shard_map/ppermute | solution.py:110
  71.1 20.6 %collective-permute-start.27 = (bf16[256,2048]{1,0:T(8,128)(2,1)S(1)}, bf16[256,2048]{1,0:T(8,128)(2,1)S(1)}, u32[]{:S(2)}, u32[]{:S(2)}) collective-permute-start(bf16[256,2048]{1,0:T(8,128)(2,1)S(1)} %shard_map.124.cot_ref.refs_6_), channel_id=1, source_target_pairs={{0,1},{1,0},{2,3},{3,2},{4,5},{5,4},{6,7},{7,6},{8,9},{9,8},{10,11... | collective-permute-start | bytes 3145736 | tf_op jit(solution)/shard_map/ppermute | solution.py:110
  75.8 25.8 %collective-permute-start.8 = (bf16[256,2048]{1,0:T(8,128)(2,1)S(1)}, bf16[256,2048]{1,0:T(8,128)(2,1)S(1)}, u32[]{:S(2)}, u32[]{:S(2)}) collective-permute-start(bf16[256,2048]{1,0:T(8,128)(2,1)S(1)} %get-tuple-element.43), channel_id=1, source_target_pairs={{0,1},{1,0},{2,3},{3,2},{4,5},{5,4},{6,7},{7,6},{8,9},{9,8},{10,11... | collective-permute-start | bytes 3145736 | tf_op jit(solution)/shard_map/ppermute | solution.py:110
  85.9 16.1 %collective-permute-start.32 = (bf16[256,2176]{1,0:T(8,128)(2,1)S(1)}, bf16[256,2176]{1,0:T(8,128)(2,1)S(1)}, u32[]{:S(2)}, u32[]{:S(2)}) collective-permute-start(bf16[256,2176]{1,0:T(8,128)(2,1)S(1)} %get-tuple-element.53), channel_id=1, source_target_pairs={{0,1},{1,0},{2,3},{3,2},{4,5},{5,4},{6,7},{7,6},{8,9},{9,8},{10,11... | collective-permute-start | bytes 3342344 | tf_op jit(solution)/shard_map/ppermute | solution.py:110
  91.6 10.8 %collective-permute-start.14 = (bf16[256,2048]{1,0:T(8,128)(2,1)S(1)}, bf16[256,2048]{1,0:T(8,128)(2,1)S(1)}, u32[]{:S(2)}, u32[]{:S(2)}) collective-permute-start(bf16[256,2048]{1,0:T(8,128)(2,1)S(1)} %get-tuple-element.45), channel_id=1, source_target_pairs={{0,1},{1,0},{2,3},{3,2},{4,5},{5,4},{6,7},{7,6},{8,9},{9,8},{10,11... | collective-permute-start | bytes 3145736 | tf_op jit(solution)/shard_map/ppermute | solution.py:110
  94.0 10.7 %collective-permute-start.28 = (bf16[256,2176]{1,0:T(8,128)(2,1)S(1)}, bf16[256,2176]{1,0:T(8,128)(2,1)S(1)}, u32[]{:S(2)}, u32[]{:S(2)}) collective-permute-start(bf16[256,2176]{1,0:T(8,128)(2,1)S(1)} %get-tuple-element.47), channel_id=1, source_target_pairs={{0,1},{1,0},{2,3},{3,2},{4,5},{5,4},{6,7},{7,6},{8,9},{9,8},{10,11... | collective-permute-start | bytes 3342344 | tf_op jit(solution)/shard_map/ppermute | solution.py:110
  102.8 35.1 %collective-permute-start.15 = (bf16[128,2048]{1,0:T(8,128)(2,1)S(1)}, bf16[128,2048]{1,0:T(8,128)(2,1)S(1)}, u32[]{:S(2)}, u32[]{:S(2)}) collective-permute-start(bf16[128,2048]{1,0:T(8,128)(2,1)S(1)} %get-tuple-element.100), channel_id=1, source_target_pairs={{0,4},{2,6},{4,0},{6,2},{8,12},{10,14},{12,8},{14,10},{16,20},{18,... | collective-permute-start | bytes 1572872 | tf_op jit(solution)/shard_map/ppermute | solution.py:125
  103.4 34.6 %collective-permute-start.29 = (bf16[128,2048]{1,0:T(8,128)(2,1)S(1)}, bf16[128,2048]{1,0:T(8,128)(2,1)S(1)}, u32[]{:S(2)}, u32[]{:S(2)}) collective-permute-start(bf16[128,2048]{1,0:T(8,128)(2,1)S(1)} %get-tuple-element.101), channel_id=1, source_target_pairs={{0,2},{2,0},{4,6},{6,4},{8,10},{10,8},{12,14},{14,12},{16,18},{18,... | collective-permute-start | bytes 1572872 | tf_op jit(solution)/shard_map/ppermute | solution.py:125
  105.0 16.1 %collective-permute-start.33 = (bf16[32,2176]{1,0:T(8,128)(2,1)S(1)}, bf16[32,2176]{1,0:T(8,128)(2,1)S(1)}, u32[]{:S(2)}, u32[]{:S(2)}) collective-permute-start(bf16[32,2176]{1,0:T(8,128)(2,1)S(1)} %pad_maximum_fusion.16), channel_id=1, source_target_pairs={{0,2},{2,0},{4,6},{6,4},{8,10},{10,8},{12,14},{14,12},{16,18},{18,... | collective-permute-start | bytes 417800 | tf_op jit(solution)/shard_map/ppermute | solution.py:125
  105.8 13.9 %collective-permute-start.40 = (bf16[32,2176]{1,0:T(8,128)(2,1)S(1)}, bf16[32,2176]{1,0:T(8,128)(2,1)S(1)}, u32[]{:S(2)}, u32[]{:S(2)}) collective-permute-start(bf16[32,2176]{1,0:T(8,128)(2,1)S(1)} %pad_maximum_fusion.17), channel_id=1, source_target_pairs={{0,4},{2,6},{4,0},{6,2},{8,12},{10,14},{12,8},{14,10},{16,20},{18,... | collective-permute-start | bytes 417800 | tf_op jit(solution)/shard_map/ppermute | solution.py:125
  107.5 28.8 %collective-permute-start.44 = (bf16[96,2176]{1,0:T(8,128)(2,1)S(1)}, bf16[96,2176]{1,0:T(8,128)(2,1)S(1)}, u32[]{:S(2)}, u32[]{:S(2)}) collective-permute-start(bf16[96,2176]{1,0:T(8,128)(2,1)S(1)} %pad_maximum_fusion.4), channel_id=1, source_target_pairs={{0,2},{2,0},{4,6},{6,4},{8,10},{10,8},{12,14},{14,12},{16,18},{18,... | collective-permute-start | bytes 1253384 | tf_op jit(solution)/shard_map/ppermute | solution.py:125
  119.8 15.0 %collective-permute-start.42 = (bf16[96,2176]{1,0:T(8,128)(2,1)S(1)}, bf16[96,2176]{1,0:T(8,128)(2,1)S(1)}, u32[]{:S(2)}, u32[]{:S(2)}) collective-permute-start(bf16[96,2176]{1,0:T(8,128)(2,1)S(1)} %pad_maximum_fusion.3), channel_id=1, source_target_pairs={{0,4},{2,6},{4,0},{6,2},{8,12},{10,14},{12,8},{14,10},{16,20},{18,... | collective-permute-start | bytes 1253384 | tf_op jit(solution)/shard_map/ppermute | solution.py:125
  121.2 9.2 %collective-permute-start.41 = (bf16[16,2176]{1,0:T(8,128)(2,1)S(1)}, bf16[16,2176]{1,0:T(8,128)(2,1)S(1)}, u32[]{:S(2)}, u32[]{:S(2)}) collective-permute-start(bf16[16,2176]{1,0:T(8,128)(2,1)S(1)} %slice.473), channel_id=1, source_target_pairs={{0,2},{2,0},{4,6},{6,4},{8,10},{10,8},{12,14},{14,12},{16,18},{18,... | collective-permute-start | bytes 208904 | tf_op jit(solution)/shard_map/ppermute | solution.py:125
  134.9 6.0 %collective-permute-start.43 = (bf16[48,2176]{1,0:T(8,128)(2,1)S(1)}, bf16[48,2176]{1,0:T(8,128)(2,1)S(1)}, u32[]{:S(2)}, u32[]{:S(2)}) collective-permute-start(bf16[48,2176]{1,0:T(8,128)(2,1)S(1)} %slice.472), channel_id=1, source_target_pairs={{0,2},{2,0},{4,6},{6,4},{8,10},{10,8},{12,14},{14,12},{16,18},{18,... | collective-permute-start | bytes 626696 | tf_op jit(solution)/shard_map/ppermute | solution.py:125
  136.4 5.9 %collective-permute-start.45 = (bf16[48,2176]{1,0:T(8,128)(2,1)S(1)}, bf16[48,2176]{1,0:T(8,128)(2,1)S(1)}, u32[]{:S(2)}, u32[]{:S(2)}) collective-permute-start(bf16[48,2176]{1,0:T(8,128)(2,1)S(1)} %slice.471), channel_id=1, source_target_pairs={{0,4},{2,6},{4,0},{6,2},{8,12},{10,14},{12,8},{14,10},{16,20},{18,... | collective-permute-start | bytes 626696 | tf_op jit(solution)/shard_map/ppermute | solution.py:125
  138.5 22.0 %collective-permute-start.35 = (bf16[64,2048]{1,0:T(8,128)(2,1)S(1)}, bf16[64,2048]{1,0:T(8,128)(2,1)S(1)}, u32[]{:S(2)}, u32[]{:S(2)}) collective-permute-start(bf16[64,2048]{1,0:T(8,128)(2,1)S(1)} %pad_maximum_fusion.8), channel_id=1, source_target_pairs={{0,24},{2,26},{4,28},{6,30},{8,0},{10,2},{12,4},{14,6},{16,8},{18,... | collective-permute-start | bytes 786440 | tf_op jit(solution)/shard_map/ppermute | solution.py:170
  138.6 21.9 %collective-permute-start.36 = (bf16[64,2048]{1,0:T(8,128)(2,1)S(1)}, bf16[64,2048]{1,0:T(8,128)(2,1)S(1)}, u32[]{:S(2)}, u32[]{:S(2)}) collective-permute-start(bf16[64,2048]{1,0:T(8,128)(2,1)S(1)} %pad_maximum_fusion.9), channel_id=1, source_target_pairs={{0,16},{2,18},{4,20},{6,22},{8,24},{10,26},{12,28},{14,30},{16,0},... | collective-permute-start | bytes 786440 | tf_op jit(solution)/shard_map/ppermute | solution.py:170
  138.8 21.8 %collective-permute-start.30 = (bf16[64,2048]{1,0:T(8,128)(2,1)S(1)}, bf16[64,2048]{1,0:T(8,128)(2,1)S(1)}, u32[]{:S(2)}, u32[]{:S(2)}) collective-permute-start(bf16[64,2048]{1,0:T(8,128)(2,1)S(1)} %pad_maximum_fusion.7), channel_id=1, source_target_pairs={{0,8},{2,10},{4,12},{6,14},{8,16},{10,18},{12,20},{14,22},{16,24},... | collective-permute-start | bytes 786440 | tf_op jit(solution)/shard_map/ppermute | solution.py:170
  142.4 27.0 %collective-permute-start.47 = (bf16[32,2176]{1,0:T(8,128)(2,1)S(1)}, bf16[32,2176]{1,0:T(8,128)(2,1)S(1)}, u32[]{:S(2)}, u32[]{:S(2)}) collective-permute-start(bf16[32,2176]{1,0:T(8,128)(2,1)S(1)} %pad_maximum_fusion.19), channel_id=1, source_target_pairs={{0,24},{2,26},{4,28},{6,30},{8,0},{10,2},{12,4},{14,6},{16,8},{18,... | collective-permute-start | bytes 417800 | tf_op jit(solution)/shard_map/ppermute | solution.py:170
  160.7 5.9 %collective-permute-start.37 = (bf16[16,2048]{1,0:T(8,128)(2,1)S(1)}, bf16[16,2048]{1,0:T(8,128)(2,1)S(1)}, u32[]{:S(2)}, u32[]{:S(2)}) collective-permute-start(bf16[16,2048]{1,0:T(8,128)(2,1)S(1)} %get-tuple-element.116), channel_id=1, source_target_pairs={{0,2},{2,0},{4,6},{6,4},{8,10},{10,8},{12,14},{14,12},{16,18},{18,... | collective-permute-start | bytes 196616 | tf_op jit(solution)/shard_map/ppermute | solution.py:125
  161.6 5.0 %collective-permute-start.38 = (bf16[16,2048]{1,0:T(8,128)(2,1)S(1)}, bf16[16,2048]{1,0:T(8,128)(2,1)S(1)}, u32[]{:S(2)}, u32[]{:S(2)}) collective-permute-start(bf16[16,2048]{1,0:T(8,128)(2,1)S(1)} %get-tuple-element.117), channel_id=1, source_target_pairs={{0,4},{2,6},{4,0},{6,2},{8,12},{10,14},{12,8},{14,10},{16,20},{18,... | collective-permute-start | bytes 196616 | tf_op jit(solution)/shard_map/ppermute | solution.py:125
  163.1 12.7 %collective-permute-start.48 = (bf16[32,2176]{1,0:T(8,128)(2,1)S(1)}, bf16[32,2176]{1,0:T(8,128)(2,1)S(1)}, u32[]{:S(2)}, u32[]{:S(2)}) collective-permute-start(bf16[32,2176]{1,0:T(8,128)(2,1)S(1)} %pad_maximum_fusion.20), channel_id=1, source_target_pairs={{0,16},{2,18},{4,20},{6,22},{8,24},{10,26},{12,28},{14,30},{16,0},... | collective-permute-start | bytes 417800 | tf_op jit(solution)/shard_map/ppermute | solution.py:170
  166.7 9.1 %collective-permute-start.46 = (bf16[32,2176]{1,0:T(8,128)(2,1)S(1)}, bf16[32,2176]{1,0:T(8,128)(2,1)S(1)}, u32[]{:S(2)}, u32[]{:S(2)}) collective-permute-start(bf16[32,2176]{1,0:T(8,128)(2,1)S(1)} %pad_maximum_fusion.18), channel_id=1, source_target_pairs={{0,8},{2,10},{4,12},{6,14},{8,16},{10,18},{12,20},{14,22},{16,24},... | collective-permute-start | bytes 417800 | tf_op jit(solution)/shard_map/ppermute | solution.py:170
  175.9 5.4 %collective-permute-start.49 = (bf16[32,2176]{1,0:T(8,128)(2,1)S(1)}, bf16[32,2176]{1,0:T(8,128)(2,1)S(1)}, u32[]{:S(2)}, u32[]{:S(2)}) collective-permute-start(bf16[32,2176]{1,0:T(8,128)(2,1)S(1)} %fusion.6), channel_id=1, source_target_pairs={{0,1},{1,0},{2,3},{3,2},{4,5},{5,4},{6,7},{7,6},{8,9},{9,8},{10,11... | collective-permute-start | bytes 417800 | tf_op jit(solution)/shard_map/ppermute | solution.py:110
  (6 other events, 39.6 us)

commit v2 on v1

--- a/solution.py
+++ b/solution.py
@@ -193,19 +193,25 @@
     pairs = fold(n, by_colour(one), by_colour(two), 1)
     parts = summed([(mine, after(moved, held)) for mine, moved in pairs])
     runs = [p[at : at + near_rows] for p in parts for at in (0, near_rows)]
+    *others, farthest = enumerate(near_first(n // 4))
     shifted = []
-    for at, j in enumerate(near_first(n // 4)):
+    for at, j in others:
         block = stack(*[run[(at + 1) * rows : (at + 2) * rows] for run in runs])
         shifted.append(shift_home(block, n, j))
-    return stack(*[run[:rows] for run in runs]), shifted
-
-
-def finish_outputs(kept, shifted, n, held):
+    at, j = farthest
+    ends = [run[(at + 1) * rows : (at + 2) * rows] for run in runs]
+    ends = stack(*summed(fold(n, ends[0::2], ends[1::2], 0)))
+    last = shift_home(ends, n, j)
+    return stack(*[run[:rows] for run in runs]), shifted, last
+
+
+def finish_outputs(kept, shifted, last, n, held):
     total = kept
     for moved in shifted:
         total = total + wide(after(moved, held))
     halves = [by_colour(part) for part in by_colour(total)]
-    return narrow(stack(*summed(fold(n, *zip(*halves), 0))))
+    total = stack(*summed(fold(n, *zip(*halves), 0)))
+    return narrow(total + wide(after(last, held)))
 
 
 def collect_gradients(one, two, n):
@@ -222,9 +228,9 @@
     far_pairs = fold(n, [far(x) for x in ones], [far(x) for x in twos], 1)
     own_pairs = fold(n, [own(x) for x in ones], [own(x) for x in twos], 1)
     far_pairs = fold(n, *zip(*[by_colour(x) for x in summed(far_pairs)]), 0)
+    mark = far_pairs[1][1]
     fars = summed(far_pairs)
     own_pairs = fold(n, *zip(*[by_colour(x) for x in summed(own_pairs)]), 0)
-    mark = own_pairs[1][1]
     total = stack(*summed(own_pairs))
     shifted = []
     for at, j in enumerate(near_first(n // 4)):
@@ -241,14 +247,14 @@
     return x.size * x.dtype.itemsize
 
 
-def whole(kernel, out_shapes, args, scalars=0, flops=0):
+def whole(kernel, out_shapes, args, scalars=0):
     moved = sum(size_of(x) for x in jax.tree.leaves((args, out_shapes)))
     return pl.pallas_call(
         kernel,
         out_shape=out_shapes,
         in_specs=[SMEM] * scalars + [VMEM] * (len(args) - scalars),
         out_specs=jax.tree.map(lambda _: VMEM, out_shapes),
-        cost_estimate=pl.CostEstimate(flops=flops, bytes_accessed=moved, transcendentals=0),
+        cost_estimate=pl.CostEstimate(flops=1000, bytes_accessed=moved, transcendentals=0),
         compiler_params=pltpu.CompilerParams(vmem_limit_bytes=moved + 4 * 2**20),
     )(*args)
 
@@ -266,13 +272,20 @@
 
     total = sum(p.shape[0] for p in parts)
     shape = jax.ShapeDtypeStruct((total, parts[0].shape[1]), parts[0].dtype)
-    return whole(kernel, shape, parts, 0, 1000 * total)
+    return whole(kernel, shape, parts, 0)
+
+
+def add_rows(x, y):
+    def kernel(x_ref, y_ref, out_ref):
+        out_ref[...] = x_ref[...] + wide(y_ref[...])
+
+    return whole(kernel, jax.ShapeDtypeStruct(x.shape, x.dtype), (x, y))
 
 
 def product_over_rows(left, right, tall=None):
     groups = len(left)
-    tile = 256
     rows, width = right[0].shape
+    tile = 256 if tall else max(t for t in (128, 256, 512, 1024) if width % t == 0)
 
     def kernel(*refs):
         def joined(k):
@@ -295,21 +308,19 @@
         in_specs = fixed(unit) + moving()
         out_shape = [jax.ShapeDtypeStruct((1, unit, features), jnp.bfloat16)]
         out_specs = [pl.BlockSpec((1, unit, tile), lambda i: (0, 0, i))]
-        flops = 2 * groups * rows * unit * features
     else:
         unit = width // 2
         features = tall
         in_specs = moving() + fixed(width)
         out_shape = [jax.ShapeDtypeStruct((1, features, unit), jnp.bfloat16)] * 2
         out_specs = [pl.BlockSpec((1, tile, unit), lambda i: (0, i, 0))] * 2
-        flops = 2 * groups * rows * width * features
     return pl.pallas_call(
         kernel,
         grid=(features // tile,),
         out_shape=out_shape,
         in_specs=in_specs,
         out_specs=out_specs,
-        cost_estimate=pl.CostEstimate(flops=flops, bytes_accessed=0, transcendentals=0),
+        cost_estimate=pl.CostEstimate(flops=1000, bytes_accessed=0, transcendentals=0),
         compiler_params=pltpu.CompilerParams(vmem_limit_bytes=14 * 2**20),
     )(*left, *right)
 
@@ -357,7 +368,7 @@
         jax.ShapeDtypeStruct((rows, unit), jnp.bfloat16),
         jax.ShapeDtypeStruct((rows, features), out_dtype),
     )
-    return whole(kernel, shapes, (where, rows_in, w_in, w_down), 1, 3 * rows * features * width)
+    return whole(kernel, shapes, (where, rows_in, w_in, w_down), 1)
 
 
 def backward(cot, rows_in, pre, w_in, w_down, where, experts, halves, out_dtype):
@@ -409,7 +420,7 @@
         jax.ShapeDtypeStruct((rows, features + back_width), out_dtype),
     )
     operands = (where, cot, rows_in, pre, w_in, w_down)
-    return whole(kernel, shapes, operands, 1, 3 * rows * features * width)
+    return whole(kernel, shapes, operands, 1)
 
 
 def pieces(x):
@@ -473,11 +484,14 @@
             all_weighted.append(weighted)
             all_cots.append(cot)
         slot_other = swap_half(slots[1])
-        slot_sums[tag] = slots[0] + wide(slot_other)
-
-    mix_kept, mix_shifted = collect_outputs(sums["f"], sums["s"], senders, slot_other)
+        if tag == "f":
+            slot_sums[tag] = add_rows(slots[0], slot_other)
+        else:
+            slot_sums[tag] = slots[0] + wide(slot_other)
+
+    mix_parts = collect_outputs(sums["f"], sums["s"], senders, slot_other)
     grad_home, grad_shifted, mark = collect_gradients(slot_sums["f"], slot_sums["s"], senders)
-    mixed = finish_outputs(mix_kept, mix_shifted, senders, mark)
+    mixed = finish_outputs(*mix_parts, senders, mark)
     (grad_down,) = product_over_rows(all_weighted, all_cots)
     grad_gate, grad_up = product_over_rows(all_rows, all_d, features)
 
@@ -486,7 +500,7 @@
 
     mixed = both(mixed, swap_half(mixed))
     for moved in grad_shifted:
-        grad_home = grad_home + wide(after(moved, mixed))
+        grad_home = grad_home + wide(moved)
     grad_home = narrow(grad_home)
     grad_other = swap_half(grad_home)
     token_grad = both(grad_home[:, :features], grad_other[:, :features])

time: 183 us -> 174 us (0.951)
  waiting for transfers between devices: 84.3 us -> 74.6 us
  starting transfers between devices: 53.8 us -> 56.3 us
    ppermute x28 -> x30, waiting for transfers between devices: 60.6 us -> 53.8 us  [flip(): return lax.ppermute(x, 'expert', flipped(n, bit))]
    ppermute x6, waiting for transfers between devices: 23.6 us -> 20 us  [shift_home(): lax.ppermute(narrow(block), 'expert', [(d, s) for s, d in rolled(n, j)])]
    ppermute x28 -> x30, starting transfers between devices: 31 us -> 34.5 us  [flip(): return lax.ppermute(x, 'expert', flipped(n, bit))]
    ppermute x6, starting transfers between devices: 8.57 us -> 6.5 us  [shift_home(): lax.ppermute(narrow(block), 'expert', [(d, s) for s, d in rolled(n, j)])]
    pallas_call x2, Pallas kernels: 12.3 us -> 10.3 us  [product_over_rows(): pl.pallas_call(kernel, grid=(features // tile,), out_shape=out_shape, in_...]
    pallas_call x12 -> x13, Pallas kernels: 20.4 us -> 20.6 us  [whole(): pl.pallas_call(kernel, out_shape=out_shapes, in_specs=[SMEM] * scalars +...]
  transfers between devices with their start and end apart: 50 -> 52, of which waited for: 14 -> 15; matrix products, arithmetic and copies ran while one was open for 4% -> 4% of each run, Pallas kernels for 18% -> 18%
where the time goes in v2:
time: 174 us
  waiting for transfers between devices  74.6 us (43%)
  starting transfers between devices  56.3 us (32%)
  Pallas kernels  30.9 us (18%)
  other arithmetic  6.62 us (4%)
  local copies, waits for them, and re-layouts  3.79 us (2%)
    ppermute x30, waiting for transfers between devices, flip(): return lax.ppermute(x, 'expert', flipped(n, bit))  53.8 us
    ppermute x30, starting transfers between devices, flip(): return lax.ppermute(x, 'expert', flipped(n, bit))  34.5 us
    pallas_call x13, Pallas kernels, whole(): pl.pallas_call(kernel, out_shape=out_shapes, in_specs=[SMEM] * scalars +...  20.6 us
    ppermute x6, waiting for transfers between devices, shift_home(): lax.ppermute(narrow(block), 'expert', [(d, s) for s, d in rolled(n, j)])  20 us
    ppermute x6, starting transfers between devices, spread(): lax.ppermute(block, 'expert', rolled(n, j))  12.2 us
    pallas_call x2, Pallas kernels, product_over_rows(): pl.pallas_call(kernel, grid=(features // tile,), out_shape=out_shape, in_...  10.3 us
    ppermute x6, starting transfers between devices, shift_home(): lax.ppermute(narrow(block), 'expert', [(d, s) for s, d in rolled(n, j)])  6.5 us
  transfers between devices with their start and end apart: 52, of which 15 were waited for; matrix products, arithmetic and copies ran while one was open for 4% of the time, Pallas kernels for 18%

profile of v2, /device:TPU:0, one launch (start us, length us, event | category | flops | bytes accessed | tf_op | source)
XLA Modules:
  0.0 173.6 jit_solution(14662659390786098554)
XLA Ops:
  1.6 3.1 %collective-permute-start.19 = (bf16[32,2048]{1,0:T(8,128)(2,1)S(1)}, bf16[32,2048]{1,0:T(8,128)(2,1)S(1)}, u32[]{:S(2)}, u32[]{:S(2)}) collective-permute-start(bf16[32,2048]{1,0:T(8,128)(2,1)S(1)} %constant_dynamic-slice_fusion.1), channel_id=1, source_target_pairs={{24,0},{26,2},{28,4},{30,6},{0,8},{2,10},{4,12},{6,14},{8,16},{10,... | collective-permute-start | bytes 393224 | tf_op jit(solution)/shard_map/ppermute | solution.py:136
  4.7 2.1 %collective-permute-start.18 = (bf16[32,2048]{1,0:T(8,128)(2,1)S(1)}, bf16[32,2048]{1,0:T(8,128)(2,1)S(1)}, u32[]{:S(2)}, u32[]{:S(2)}) collective-permute-start(bf16[32,2048]{1,0:T(8,128)(2,1)S(1)} %constant_dynamic-slice_fusion.1), channel_id=1, source_target_pairs={{8,0},{10,2},{12,4},{14,6},{16,8},{18,10},{20,12},{22,14},{24,16},... | collective-permute-start | bytes 393224 | tf_op jit(solution)/shard_map/ppermute | solution.py:136
  6.8 0.9 collective-permute-start.20
  8.6 1.6 collective-permute-start.16
  12.2 2.2 %collective-permute-start.2 = (bf16[32,2176]{1,0:T(8,128)(2,1)S(1)}, bf16[32,2176]{1,0:T(8,128)(2,1)S(1)}, u32[]{:S(2)}, u32[]{:S(2)}) collective-permute-start(bf16[32,2176]{1,0:T(8,128)(2,1)S(1)} %fusion.7), channel_id=1, source_target_pairs={{16,0},{18,2},{20,4},{22,6},{24,8},{26,10},{28,12},{30,14},{0,16},... | collective-permute-start | bytes 417800 | tf_op jit(solution)/shard_map/ppermute | solution.py:136
  14.4 1.6 collective-permute-start.23
  16.0 2.7 %collective-permute-done.23.refs_6_ = bf16[16,2048]{1,0:T(8,128)(2,1)S(1)} collective-permute-done((bf16[16,2048]{1,0:T(8,128)(2,1)S(1)}, bf16[16,2048]{1,0:T(8,128)(2,1)S(1)}, u32[]{:S(2)}, u32[]{:S(2)}) %collective-permute-start.23) | collective-permute-done | bytes 65568 | tf_op jit(solution)/shard_map/ppermute | solution.py:125
  18.7 1.5 collective-permute-start.5
  20.2 2.8 %collective-permute-done.5.refs_6_ = bf16[16,2176]{1,0:T(8,128)(2,1)S(1)} collective-permute-done((bf16[16,2176]{1,0:T(8,128)(2,1)S(1)}, bf16[16,2176]{1,0:T(8,128)(2,1)S(1)}, u32[]{:S(2)}, u32[]{:S(2)}) %collective-permute-start.5) | collective-permute-done | bytes 69664 | tf_op jit(solution)/shard_map/ppermute | solution.py:125
  23.2 3.7 %collective-permute-start = (bf16[32,2176]{1,0:T(8,128)(2,1)S(1)}, bf16[32,2176]{1,0:T(8,128)(2,1)S(1)}, u32[]{:S(2)}, u32[]{:S(2)}) collective-permute-start(bf16[32,2176]{1,0:T(8,128)(2,1)S(1)} %fusion.7), channel_id=1, source_target_pairs={{8,0},{10,2},{12,4},{14,6},{16,8},{18,10},{20,12},{22,14},{24,16},... | collective-permute-start | bytes 417800 | tf_op jit(solution)/shard_map/ppermute | solution.py:136
  27.4 1.7 collective-permute-start.24
  29.2 1.6 collective-permute-start.17
  32.2 4.4 %collective-permute-done.21.refs_3_ = bf16[48,2048]{1,0:T(8,128)(2,1)S(1)} collective-permute-done((bf16[48,2048]{1,0:T(8,128)(2,1)S(1)}, bf16[48,2048]{1,0:T(8,128)(2,1)S(1)}, u32[]{:S(2)}, u32[]{:S(2)}) %collective-permute-start.21) | collective-permute-done | bytes 196640 | tf_op jit(solution)/shard_map/ppermute | solution.py:125
  37.4 1.3 collective-permute-start.6
  38.7 4.9 %collective-permute-done.4.refs_3_ = bf16[48,2176]{1,0:T(8,128)(2,1)S(1)} collective-permute-done((bf16[48,2176]{1,0:T(8,128)(2,1)S(1)}, bf16[48,2176]{1,0:T(8,128)(2,1)S(1)}, u32[]{:S(2)}, u32[]{:S(2)}) %collective-permute-start.4) | collective-permute-done | bytes 208928 | tf_op jit(solution)/shard_map/ppermute | solution.py:125
  44.0 1.8 %collective-permute-start.11 = (bf16[32,2176]{1,0:T(8,128)(2,1)S(1)}, bf16[32,2176]{1,0:T(8,128)(2,1)S(1)}, u32[]{:S(2)}, u32[]{:S(2)}) collective-permute-start(bf16[32,2176]{1,0:T(8,128)(2,1)S(1)} %pad_maximum_fusion.14), channel_id=1, source_target_pairs={{0,2},{2,0},{4,6},{6,4},{8,10},{10,8},{12,14},{14,12},{16,18},{18,... | collective-permute-start | bytes 417800 | tf_op jit(solution)/shard_map/ppermute | solution.py:125
  45.8 1.7 collective-permute-start.22
  48.2 7.7 %collective-permute-done.11.refs_2_ = bf16[32,2176]{1,0:T(8,128)(2,1)S(1)} collective-permute-done((bf16[32,2176]{1,0:T(8,128)(2,1)S(1)}, bf16[32,2176]{1,0:T(8,128)(2,1)S(1)}, u32[]{:S(2)}, u32[]{:S(2)}) %collective-permute-start.11) | collective-permute-done | bytes 139296 | tf_op jit(solution)/shard_map/ppermute | solution.py:125
  56.2 1.5 collective-permute-start.10
  58.4 7.3 %collective-permute-done.9.refs_0_ = bf16[32,2176]{1,0:T(8,128)(2,1)S(1)} collective-permute-done((bf16[32,2176]{1,0:T(8,128)(2,1)S(1)}, bf16[32,2176]{1,0:T(8,128)(2,1)S(1)}, u32[]{:S(2)}, u32[]{:S(2)}) %collective-permute-start.9) | collective-permute-done | bytes 139296 | tf_op jit(solution)/shard_map/ppermute | solution.py:125
  66.7 1.1 copy-done
  67.8 2.7 %shard_map.120 = (f32[256,768]{1,0:T(8,128)S(1)}, bf16[256,384]{1,0:T(8,128)(2,1)S(1)}, bf16[256,2048]{1,0:T(8,128)(2,1)S(1)}) custom-call(s32[2]{0:T(128)S(1)} %pad_add_fusion.where_ref, bf16[256,2176]{1,0:T(8,128)(2,1)S(1)} %collective-permute-done.7.x_ref.side_ref.refs_1_, bf16[2048,768]{1,0:T(8,128)(2,1)S(1)} %pad_maximum_fusion.win_ref, ...), custom_call_target="tpu_custom_call" | custom-call | flops 1000 | bytes 7864328 | tf_op jit(solution)/shard_map/pallas_call | solution.py:252
  70.6 2.3 %shard_map.128 = (bf16[256,768]{1,0:T(8,128)(2,1)S(1)}, bf16[256,2176]{1,0:T(8,128)(2,1)S(1)}) custom-call(s32[2]{0:T(128)S(1)} %pad_add_fusion.where_ref, bf16[256,2048]{1,0:T(8,128)(2,1)S(1)} %collective-permute-done.31.cot_ref.refs_5_, bf16[256,2176]{1,0:T(8,128)(2,1)S(1)} %collective-permute-done.7.x_ref.side_ref.refs_1_, ...), custom_call_target="tpu_custom_call" | custom-call | flops 1000 | bytes 9175048 | tf_op jit(solution)/shard_map/pallas_call | solution.py:252
  73.5 2.7 %shard_map.119 = (f32[256,768]{1,0:T(8,128)S(1)}, bf16[256,384]{1,0:T(8,128)(2,1)S(1)}, f32[256,2048]{1,0:T(8,128)S(1)}) custom-call(s32[2]{0:T(128)S(1)} %pad_add_fusion.where_ref, bf16[256,2176]{1,0:T(8,128)(2,1)S(1)} %shard_map.118.x_ref.side_ref.refs_0_, bf16[2048,768]{1,0:T(8,128)(2,1)S(1)} %pad_maximum_fusion.win_ref, bf16[384,2048]{1,0:T(8,128)(2,1)S(1)} %bitcast.8), custom_call_target="tpu_custom_call" | custom-call | flops 1000 | bytes 8912904 | tf_op jit(solution)/shard_map/pallas_call | solution.py:252
  76.2 2.3 %shard_map.127 = (bf16[256,768]{1,0:T(8,128)(2,1)S(1)}, f32[256,2176]{1,0:T(8,128)S(1)}) custom-call(s32[2]{0:T(128)S(1)} %pad_add_fusion.where_ref, bf16[256,2048]{1,0:T(8,128)(2,1)S(1)} %shard_map.126.cot_ref.refs_4_, bf16[256,2176]{1,0:T(8,128)(2,1)S(1)} %shard_map.118.x_ref.side_ref.refs_0_, f32[256,768]{1,0:T(8,128)S(1)} %get-tuple-element.47.pre_ref, ...), custom_call_target="tpu_custom_call" | custom-call | flops 1000 | bytes 10289160 | tf_op jit(solution)/shard_map/pallas_call | solution.py:252
  78.5 2.7 %shard_map.122 = (f32[256,768]{1,0:T(8,128)S(1)}, bf16[256,384]{1,0:T(8,128)(2,1)S(1)}, f32[256,2048]{1,0:T(8,128)S(1)}) custom-call(s32[2]{0:T(128)S(1)} %pad_add_fusion.where_ref, bf16[256,2176]{1,0:T(8,128)(2,1)S(1)} %shard_map.121.x_ref.side_ref.refs_2_, bf16[2048,768]{1,0:T(8,128)(2,1)S(1)} %pad_maximum_fusion.win_ref, bf16[384,2048]{1,0:T(8,128)(2,1)S(1)} %bitcast.10), custom_call_target="tpu_custom_call" | custom-call | flops 1000 | bytes 8912904 | tf_op jit(solution)/shard_map/pallas_call | solution.py:252
  81.2 2.3 %shard_map.130 = (bf16[256,768]{1,0:T(8,128)(2,1)S(1)}, f32[256,2176]{1,0:T(8,128)S(1)}) custom-call(s32[2]{0:T(128)S(1)} %pad_add_fusion.where_ref, bf16[256,2048]{1,0:T(8,128)(2,1)S(1)} %shard_map.124.cot_ref.refs_6_, bf16[256,2176]{1,0:T(8,128)(2,1)S(1)} %shard_map.121.x_ref.side_ref.refs_2_, f32[256,768]{1,0:T(8,128)S(1)} %get-tuple-element.51.pre_ref, ...), custom_call_target="tpu_custom_call" | custom-call | flops 1000 | bytes 10289160 | tf_op jit(solution)/shard_map/pallas_call | solution.py:252
  83.5 2.9 %shard_map.123 = (f32[256,768]{1,0:T(8,128)S(1)}, bf16[256,384]{1,0:T(8,128)(2,1)S(1)}, bf16[256,2048]{1,0:T(8,128)(2,1)S(1)}) custom-call(s32[2]{0:T(128)S(1)} %pad_add_fusion.where_ref, bf16[256,2176]{1,0:T(8,128)(2,1)S(1)} %collective-permute-done.13.x_ref.side_ref.refs_3_, bf16[2048,768]{1,0:T(8,128)(2,1)S(1)} %pad_maximum_fusion.win_ref, ...), custom_call_target="tpu_custom_call" | custom-call | flops 1000 | bytes 7864328 | tf_op jit(solution)/shard_map/pallas_call | solution.py:252
  86.5 2.3 %shard_map.125 = (bf16[256,768]{1,0:T(8,128)(2,1)S(1)}, bf16[256,2176]{1,0:T(8,128)(2,1)S(1)}) custom-call(s32[2]{0:T(128)S(1)} %pad_add_fusion.where_ref, bf16[256,2048]{1,0:T(8,128)(2,1)S(1)} %collective-permute-done.27.cot_ref.refs_7_, bf16[256,2176]{1,0:T(8,128)(2,1)S(1)} %collective-permute-done.13.x_ref.side_ref.refs_3_, ...), custom_call_target="tpu_custom_call" | custom-call | flops 1000 | bytes 9175048 | tf_op jit(solution)/shard_map/pallas_call | solution.py:252
  89.3 3.2 %shard_map.132 = bf16[1,384,2048]{2,1,0:T(8,128)(2,1)} custom-call(bf16[256,384]{1,0:T(8,128)(2,1)S(1)} %get-tuple-element.62.refs_0_, bf16[256,384]{1,0:T(8,128)(2,1)S(1)} %get-tuple-element.63.refs_1_, bf16[256,384]{1,0:T(8,128)(2,1)S(1)} %get-tuple-element.64.refs_2_, bf16[256,384]{1,0:T(8,128)(2,1)S(1)} %get-tuple-element.65.refs_3_, ...), custom_call_target="tpu_custom_call" | custom-call | flops 1000 | tf_op jit(solution)/shard_map/pallas_call | solution.py:317
  92.5 7.1 %shard_map.131 = (bf16[1,2048,384]{2,1,0:T(8,128)(2,1)}, bf16[1,2048,384]{2,1,0:T(8,128)(2,1)}) custom-call(bf16[256,2176]{1,0:T(8,128)(2,1)S(1)} %shard_map.118.x_ref.side_ref.refs_0_, bf16[256,2176]{1,0:T(8,128)(2,1)S(1)} %collective-permute-done.7.x_ref.side_ref.refs_1_, bf16[256,2176]{1,0:T(8,128)(2,1)S(1)} %shard_map.121.x_ref.side_ref.refs_2_, ...), custom_call_target="tpu_custom_call" | custom-call | flops 1000 | tf_op jit(solution)/shard_map/pallas_call | solution.py:317
  100.8 1.6 collective-permute-start.15
  102.4 1.9 %collective-permute-start.29 = (bf16[128,2048]{1,0:T(8,128)(2,1)S(1)}, bf16[128,2048]{1,0:T(8,128)(2,1)S(1)}, u32[]{:S(2)}, u32[]{:S(2)}) collective-permute-start(bf16[128,2048]{1,0:T(8,128)(2,1)S(1)} %get-tuple-element.97), channel_id=1, source_target_pairs={{0,2},{2,0},{4,6},{6,4},{8,10},{10,8},{12,14},{14,12},{16,18},{18,... | collective-permute-start | bytes 1572872 | tf_op jit(solution)/shard_map/ppermute | solution.py:125
  105.4 1.8 %collective-permute-start.33 = (bf16[96,2176]{1,0:T(8,128)(2,1)S(1)}, bf16[96,2176]{1,0:T(8,128)(2,1)S(1)}, u32[]{:S(2)}, u32[]{:S(2)}) collective-permute-start(bf16[96,2176]{1,0:T(8,128)(2,1)S(1)} %pad_maximum_fusion.3), channel_id=1, source_target_pairs={{0,2},{2,0},{4,6},{6,4},{8,10},{10,8},{12,14},{14,12},{16,18},{18,... | collective-permute-start | bytes 1253384 | tf_op jit(solution)/shard_map/ppermute | solution.py:125
  107.2 10.5 %collective-permute-done.42 = bf16[32,2176]{1,0:T(8,128)(2,1)S(1)} collective-permute-done((bf16[32,2176]{1,0:T(8,128)(2,1)S(1)}, bf16[32,2176]{1,0:T(8,128)(2,1)S(1)}, u32[]{:S(2)}, u32[]{:S(2)}) %collective-permute-start.42) | collective-permute-done | bytes 139296 | tf_op jit(solution)/shard_map/ppermute | solution.py:125
  117.7 1.5 collective-permute-start.46
  120.2 1.9 %collective-permute-start.43 = (bf16[16,2176]{1,0:T(8,128)(2,1)S(1)}, bf16[16,2176]{1,0:T(8,128)(2,1)S(1)}, u32[]{:S(2)}, u32[]{:S(2)}) collective-permute-start(bf16[16,2176]{1,0:T(8,128)(2,1)S(1)} %slice.474), channel_id=1, source_target_pairs={{0,2},{2,0},{4,6},{6,4},{8,10},{10,8},{12,14},{14,12},{16,18},{18,... | collective-permute-start | bytes 208904 | tf_op jit(solution)/shard_map/ppermute | solution.py:125
  122.1 7.4 %collective-permute-done.43 = bf16[16,2176]{1,0:T(8,128)(2,1)S(1)} collective-permute-done((bf16[16,2176]{1,0:T(8,128)(2,1)S(1)}, bf16[16,2176]{1,0:T(8,128)(2,1)S(1)}, u32[]{:S(2)}, u32[]{:S(2)}) %collective-permute-start.43) | collective-permute-done | bytes 69664 | tf_op jit(solution)/shard_map/ppermute | solution.py:125
  129.9 3.9 %collective-permute-done.45 = bf16[16,2176]{1,0:T(8,128)(2,1)S(1)} collective-permute-done((bf16[16,2176]{1,0:T(8,128)(2,1)S(1)}, bf16[16,2176]{1,0:T(8,128)(2,1)S(1)}, u32[]{:S(2)}, u32[]{:S(2)}) %collective-permute-start.45) | collective-permute-done | bytes 69664 | tf_op jit(solution)/shard_map/ppermute | solution.py:125
  134.0 1.8 %collective-permute-start.47 = (bf16[48,2176]{1,0:T(8,128)(2,1)S(1)}, bf16[48,2176]{1,0:T(8,128)(2,1)S(1)}, u32[]{:S(2)}, u32[]{:S(2)}) collective-permute-start(bf16[48,2176]{1,0:T(8,128)(2,1)S(1)} %slice.471), channel_id=1, source_target_pairs={{0,2},{2,0},{4,6},{6,4},{8,10},{10,8},{12,14},{14,12},{16,18},{18,... | collective-permute-start | bytes 626696 | tf_op jit(solution)/shard_map/ppermute | solution.py:125
  137.2 1.7 collective-permute-start.39
  139.9 1.2 collective-permute-done.38
  141.2 1.8 %collective-permute-start.35 = (bf16[64,2048]{1,0:T(8,128)(2,1)S(1)}, bf16[64,2048]{1,0:T(8,128)(2,1)S(1)}, u32[]{:S(2)}, u32[]{:S(2)}) collective-permute-start(bf16[64,2048]{1,0:T(8,128)(2,1)S(1)} %pad_maximum_fusion.8), channel_id=1, source_target_pairs={{0,24},{2,26},{4,28},{6,30},{8,0},{10,2},{12,4},{14,6},{16,8},{18,... | collective-permute-start | bytes 786440 | tf_op jit(solution)/shard_map/ppermute | solution.py:170
  143.9 2.1 %collective-permute-start.49 = (bf16[32,2176]{1,0:T(8,128)(2,1)S(1)}, bf16[32,2176]{1,0:T(8,128)(2,1)S(1)}, u32[]{:S(2)}, u32[]{:S(2)}) collective-permute-start(bf16[32,2176]{1,0:T(8,128)(2,1)S(1)} %pad_maximum_fusion.18), channel_id=1, source_target_pairs={{0,24},{2,26},{4,28},{6,30},{8,0},{10,2},{12,4},{14,6},{16,8},{18,... | collective-permute-start | bytes 417800 | tf_op jit(solution)/shard_map/ppermute | solution.py:170
  146.4 16.5 %collective-permute-done.40 = bf16[32,2048]{1,0:T(8,128)(2,1)S(1)} collective-permute-done((bf16[32,2048]{1,0:T(8,128)(2,1)S(1)}, bf16[32,2048]{1,0:T(8,128)(2,1)S(1)}, u32[]{:S(2)}, u32[]{:S(2)}) %collective-permute-start.40) | collective-permute-done | bytes 131104 | tf_op jit(solution)/shard_map/ppermute | solution.py:170
  163.8 1.7 %collective-permute-start.36 = (bf16[16,2048]{1,0:T(8,128)(2,1)S(1)}, bf16[16,2048]{1,0:T(8,128)(2,1)S(1)}, u32[]{:S(2)}, u32[]{:S(2)}) collective-permute-start(bf16[16,2048]{1,0:T(8,128)(2,1)S(1)} %get-tuple-element.110), channel_id=1, source_target_pairs={{0,2},{2,0},{4,6},{6,4},{8,10},{10,8},{12,14},{14,12},{16,18},{18,... | collective-permute-start | bytes 196616 | tf_op jit(solution)/shard_map/ppermute | solution.py:125
  166.3 1.1 collective-permute-done.50
  167.4 2.4 %collective-permute-done.48 = bf16[32,2176]{1,0:T(8,128)(2,1)S(1)} collective-permute-done((bf16[32,2176]{1,0:T(8,128)(2,1)S(1)}, bf16[32,2176]{1,0:T(8,128)(2,1)S(1)}, u32[]{:S(2)}, u32[]{:S(2)}) %collective-permute-start.48) | collective-permute-done | bytes 139296 | tf_op jit(solution)/shard_map/ppermute | solution.py:170
  (161 shorter events, 23.9 us)
Async XLA Ops:
  1.6 21.6 %collective-permute-start.19 = (bf16[32,2048]{1,0:T(8,128)(2,1)S(1)}, bf16[32,2048]{1,0:T(8,128)(2,1)S(1)}, u32[]{:S(2)}, u32[]{:S(2)}) collective-permute-start(bf16[32,2048]{1,0:T(8,128)(2,1)S(1)} %constant_dynamic-slice_fusion.1), channel_id=1, source_target_pairs={{24,0},{26,2},{28,4},{30,6},{0,8},{2,10},{4,12},{6,14},{8,16},{10,... | collective-permute-start | bytes 393224 | tf_op jit(solution)/shard_map/ppermute | solution.py:136
  4.7 22.3 %collective-permute-start.18 = (bf16[32,2048]{1,0:T(8,128)(2,1)S(1)}, bf16[32,2048]{1,0:T(8,128)(2,1)S(1)}, u32[]{:S(2)}, u32[]{:S(2)}) collective-permute-start(bf16[32,2048]{1,0:T(8,128)(2,1)S(1)} %constant_dynamic-slice_fusion.1), channel_id=1, source_target_pairs={{8,0},{10,2},{12,4},{14,6},{16,8},{18,10},{20,12},{22,14},{24,16},... | collective-permute-start | bytes 393224 | tf_op jit(solution)/shard_map/ppermute | solution.py:136
  6.8 20.6 %collective-permute-start.20 = (bf16[32,2048]{1,0:T(8,128)(2,1)S(1)}, bf16[32,2048]{1,0:T(8,128)(2,1)S(1)}, u32[]{:S(2)}, u32[]{:S(2)}) collective-permute-start(bf16[32,2048]{1,0:T(8,128)(2,1)S(1)} %constant_dynamic-slice_fusion.1), channel_id=1, source_target_pairs={{16,0},{18,2},{20,4},{22,6},{24,8},{26,10},{28,12},{30,14},{0,16},... | collective-permute-start | bytes 393224 | tf_op jit(solution)/shard_map/ppermute | solution.py:136
  8.6 5.8 %collective-permute-start.16 = (bf16[16,2048]{1,0:T(8,128)(2,1)S(1)}, bf16[16,2048]{1,0:T(8,128)(2,1)S(1)}, u32[]{:S(2)}, u32[]{:S(2)}) collective-permute-start(bf16[16,2048]{1,0:T(8,128)(2,1)S(1)} %get-tuple-element.113.refs_0_), channel_id=1, source_target_pairs={{0,2},{2,0},{4,6},{6,4},{8,10},{10,8},{12,14},{14,12},{16,18},{18,... | collective-permute-start | bytes 196616 | tf_op jit(solution)/shard_map/ppermute | solution.py:125
  12.2 17.0 %collective-permute-start.2 = (bf16[32,2176]{1,0:T(8,128)(2,1)S(1)}, bf16[32,2176]{1,0:T(8,128)(2,1)S(1)}, u32[]{:S(2)}, u32[]{:S(2)}) collective-permute-start(bf16[32,2176]{1,0:T(8,128)(2,1)S(1)} %fusion.7), channel_id=1, source_target_pairs={{16,0},{18,2},{20,4},{22,6},{24,8},{26,10},{28,12},{30,14},{0,16},... | collective-permute-start | bytes 417800 | tf_op jit(solution)/shard_map/ppermute | solution.py:136
  14.4 4.3 %collective-permute-start.23 = (bf16[16,2048]{1,0:T(8,128)(2,1)S(1)}, bf16[16,2048]{1,0:T(8,128)(2,1)S(1)}, u32[]{:S(2)}, u32[]{:S(2)}) collective-permute-start(bf16[16,2048]{1,0:T(8,128)(2,1)S(1)} %get-tuple-element.112.refs_4_), channel_id=1, source_target_pairs={{0,4},{2,6},{4,0},{6,2},{8,12},{10,14},{12,8},{14,10},{16,20},{18,... | collective-permute-start | bytes 196616 | tf_op jit(solution)/shard_map/ppermute | solution.py:125
  23.0 7.8 %collective-permute-start.1 = (bf16[32,2176]{1,0:T(8,128)(2,1)S(1)}, bf16[32,2176]{1,0:T(8,128)(2,1)S(1)}, u32[]{:S(2)}, u32[]{:S(2)}) collective-permute-start(bf16[32,2176]{1,0:T(8,128)(2,1)S(1)} %fusion.7), channel_id=1, source_target_pairs={{24,0},{26,2},{28,4},{30,6},{0,8},{2,10},{4,12},{6,14},{8,16},{10,... | collective-permute-start | bytes 417800 | tf_op jit(solution)/shard_map/ppermute | solution.py:136
  23.2 8.2 %collective-permute-start = (bf16[32,2176]{1,0:T(8,128)(2,1)S(1)}, bf16[32,2176]{1,0:T(8,128)(2,1)S(1)}, u32[]{:S(2)}, u32[]{:S(2)}) collective-permute-start(bf16[32,2176]{1,0:T(8,128)(2,1)S(1)} %fusion.7), channel_id=1, source_target_pairs={{8,0},{10,2},{12,4},{14,6},{16,8},{18,10},{20,12},{22,14},{24,16},... | collective-permute-start | bytes 417800 | tf_op jit(solution)/shard_map/ppermute | solution.py:136
  26.9 17.1 %collective-permute-start.3 = (bf16[16,2176]{1,0:T(8,128)(2,1)S(1)}, bf16[16,2176]{1,0:T(8,128)(2,1)S(1)}, u32[]{:S(2)}, u32[]{:S(2)}) collective-permute-start(bf16[16,2176]{1,0:T(8,128)(2,1)S(1)} %get-tuple-element.127.refs_0_), channel_id=1, source_target_pairs={{0,2},{2,0},{4,6},{6,4},{8,10},{10,8},{12,14},{14,12},{16,18},{18,... | collective-permute-start | bytes 208904 | tf_op jit(solution)/shard_map/ppermute | solution.py:125
  27.4 20.1 %collective-permute-start.24 = (bf16[32,2048]{1,0:T(8,128)(2,1)S(1)}, bf16[32,2048]{1,0:T(8,128)(2,1)S(1)}, u32[]{:S(2)}, u32[]{:S(2)}) collective-permute-start(bf16[32,2048]{1,0:T(8,128)(2,1)S(1)} %pad_maximum_fusion.21), channel_id=1, source_target_pairs={{0,2},{2,0},{4,6},{6,4},{8,10},{10,8},{12,14},{14,12},{16,18},{18,... | collective-permute-start | bytes 393224 | tf_op jit(solution)/shard_map/ppermute | solution.py:125
  29.2 18.5 %collective-permute-start.17 = (bf16[32,2048]{1,0:T(8,128)(2,1)S(1)}, bf16[32,2048]{1,0:T(8,128)(2,1)S(1)}, u32[]{:S(2)}, u32[]{:S(2)}) collective-permute-start(bf16[32,2048]{1,0:T(8,128)(2,1)S(1)} %pad_maximum_fusion.20), channel_id=1, source_target_pairs={{0,4},{2,6},{4,0},{6,2},{8,12},{10,14},{12,8},{14,10},{16,20},{18,... | collective-permute-start | bytes 393224 | tf_op jit(solution)/shard_map/ppermute | solution.py:125
  30.8 5.8 %collective-permute-start.21 = (bf16[48,2048]{1,0:T(8,128)(2,1)S(1)}, bf16[48,2048]{1,0:T(8,128)(2,1)S(1)}, u32[]{:S(2)}, u32[]{:S(2)}) collective-permute-start(bf16[48,2048]{1,0:T(8,128)(2,1)S(1)} %pad_maximum_fusion.11.refs_1_), channel_id=1, source_target_pairs={{0,2},{2,0},{4,6},{6,4},{8,10},{10,8},{12,14},{14,12},{16,18},{18,... | collective-permute-start | bytes 589832 | tf_op jit(solution)/shard_map/ppermute | solution.py:125
  31.4 5.9 %collective-permute-start.25 = (bf16[48,2048]{1,0:T(8,128)(2,1)S(1)}, bf16[48,2048]{1,0:T(8,128)(2,1)S(1)}, u32[]{:S(2)}, u32[]{:S(2)}) collective-permute-start(bf16[48,2048]{1,0:T(8,128)(2,1)S(1)} %pad_maximum_fusion.12.refs_5_), channel_id=1, source_target_pairs={{0,4},{2,6},{4,0},{6,2},{8,12},{10,14},{12,8},{14,10},{16,20},{18,... | collective-permute-start | bytes 589832 | tf_op jit(solution)/shard_map/ppermute | solution.py:125
  36.6 7.0 %collective-permute-start.4 = (bf16[48,2176]{1,0:T(8,128)(2,1)S(1)}, bf16[48,2176]{1,0:T(8,128)(2,1)S(1)}, u32[]{:S(2)}, u32[]{:S(2)}) collective-permute-start(bf16[48,2176]{1,0:T(8,128)(2,1)S(1)} %pad_maximum_fusion.9.refs_1_), channel_id=1, source_target_pairs={{0,2},{2,0},{4,6},{6,4},{8,10},{10,8},{12,14},{14,12},{16,18},{18,... | collective-permute-start | bytes 626696 | tf_op jit(solution)/shard_map/ppermute | solution.py:125
  37.4 8.4 %collective-permute-start.6 = (bf16[48,2176]{1,0:T(8,128)(2,1)S(1)}, bf16[48,2176]{1,0:T(8,128)(2,1)S(1)}, u32[]{:S(2)}, u32[]{:S(2)}) collective-permute-start(bf16[48,2176]{1,0:T(8,128)(2,1)S(1)} %pad_maximum_fusion.10.refs_5_), channel_id=1, source_target_pairs={{0,4},{2,6},{4,0},{6,2},{8,12},{10,14},{12,8},{14,10},{16,20},{18,... | collective-permute-start | bytes 626696 | tf_op jit(solution)/shard_map/ppermute | solution.py:125
  43.6 12.6 %collective-permute-start.26 = (bf16[96,2048]{1,0:T(8,128)(2,1)S(1)}, bf16[96,2048]{1,0:T(8,128)(2,1)S(1)}, u32[]{:S(2)}, u32[]{:S(2)}) collective-permute-start(bf16[96,2048]{1,0:T(8,128)(2,1)S(1)} %pad_maximum_fusion.6), channel_id=1, source_target_pairs={{0,2},{2,0},{4,6},{6,4},{8,10},{10,8},{12,14},{14,12},{16,18},{18,... | collective-permute-start | bytes 1179656 | tf_op jit(solution)/shard_map/ppermute | solution.py:125
  44.0 11.9 %collective-permute-start.11 = (bf16[32,2176]{1,0:T(8,128)(2,1)S(1)}, bf16[32,2176]{1,0:T(8,128)(2,1)S(1)}, u32[]{:S(2)}, u32[]{:S(2)}) collective-permute-start(bf16[32,2176]{1,0:T(8,128)(2,1)S(1)} %pad_maximum_fusion.14), channel_id=1, source_target_pairs={{0,2},{2,0},{4,6},{6,4},{8,10},{10,8},{12,14},{14,12},{16,18},{18,... | collective-permute-start | bytes 417800 | tf_op jit(solution)/shard_map/ppermute | solution.py:125
  45.8 12.0 %collective-permute-start.22 = (bf16[96,2048]{1,0:T(8,128)(2,1)S(1)}, bf16[96,2048]{1,0:T(8,128)(2,1)S(1)}, u32[]{:S(2)}, u32[]{:S(2)}) collective-permute-start(bf16[96,2048]{1,0:T(8,128)(2,1)S(1)} %pad_maximum_fusion.5), channel_id=1, source_target_pairs={{0,4},{2,6},{4,0},{6,2},{8,12},{10,14},{12,8},{14,10},{16,20},{18,... | collective-permute-start | bytes 1179656 | tf_op jit(solution)/shard_map/ppermute | solution.py:125
  47.5 19.1 %collective-permute-start.7 = (bf16[256,2176]{1,0:T(8,128)(2,1)S(1)}, bf16[256,2176]{1,0:T(8,128)(2,1)S(1)}, u32[]{:S(2)}, u32[]{:S(2)}) collective-permute-start(bf16[256,2176]{1,0:T(8,128)(2,1)S(1)} %shard_map.118.x_ref.side_ref.refs_0_), channel_id=1, source_target_pairs={{0,1},{1,0},{2,3},{3,2},{4,5},{5,4},{6,7},{7,6},{8,9},{9,8},{10,11... | collective-permute-start | bytes 3342344 | tf_op jit(solution)/shard_map/ppermute | solution.py:110
  47.7 23.0 %collective-permute-start.31 = (bf16[256,2048]{1,0:T(8,128)(2,1)S(1)}, bf16[256,2048]{1,0:T(8,128)(2,1)S(1)}, u32[]{:S(2)}, u32[]{:S(2)}) collective-permute-start(bf16[256,2048]{1,0:T(8,128)(2,1)S(1)} %shard_map.126.cot_ref.refs_4_), channel_id=1, source_target_pairs={{0,1},{1,0},{2,3},{3,2},{4,5},{5,4},{6,7},{7,6},{8,9},{9,8},{10,11... | collective-permute-start | bytes 3145736 | tf_op jit(solution)/shard_map/ppermute | solution.py:110
  55.9 9.9 %collective-permute-start.12 = (bf16[96,2176]{1,0:T(8,128)(2,1)S(1)}, bf16[96,2176]{1,0:T(8,128)(2,1)S(1)}, u32[]{:S(2)}, u32[]{:S(2)}) collective-permute-start(bf16[96,2176]{1,0:T(8,128)(2,1)S(1)} %pad_maximum_fusion.2), channel_id=1, source_target_pairs={{0,2},{2,0},{4,6},{6,4},{8,10},{10,8},{12,14},{14,12},{16,18},{18,... | collective-permute-start | bytes 1253384 | tf_op jit(solution)/shard_map/ppermute | solution.py:125
  56.2 9.5 %collective-permute-start.10 = (bf16[96,2176]{1,0:T(8,128)(2,1)S(1)}, bf16[96,2176]{1,0:T(8,128)(2,1)S(1)}, u32[]{:S(2)}, u32[]{:S(2)}) collective-permute-start(bf16[96,2176]{1,0:T(8,128)(2,1)S(1)} %pad_maximum_fusion.1), channel_id=1, source_target_pairs={{0,4},{2,6},{4,0},{6,2},{8,12},{10,14},{12,8},{14,10},{16,20},{18,... | collective-permute-start | bytes 1253384 | tf_op jit(solution)/shard_map/ppermute | solution.py:125
  57.8 8.0 %collective-permute-start.9 = (bf16[32,2176]{1,0:T(8,128)(2,1)S(1)}, bf16[32,2176]{1,0:T(8,128)(2,1)S(1)}, u32[]{:S(2)}, u32[]{:S(2)}) collective-permute-start(bf16[32,2176]{1,0:T(8,128)(2,1)S(1)} %pad_maximum_fusion.13), channel_id=1, source_target_pairs={{0,4},{2,6},{4,0},{6,2},{8,12},{10,14},{12,8},{14,10},{16,20},{18,... | collective-permute-start | bytes 417800 | tf_op jit(solution)/shard_map/ppermute | solution.py:125
  65.8 20.7 %collective-permute-start.27 = (bf16[256,2048]{1,0:T(8,128)(2,1)S(1)}, bf16[256,2048]{1,0:T(8,128)(2,1)S(1)}, u32[]{:S(2)}, u32[]{:S(2)}) collective-permute-start(bf16[256,2048]{1,0:T(8,128)(2,1)S(1)} %shard_map.124.cot_ref.refs_6_), channel_id=1, source_target_pairs={{0,1},{1,0},{2,3},{3,2},{4,5},{5,4},{6,7},{7,6},{8,9},{9,8},{10,11... | collective-permute-start | bytes 3145736 | tf_op jit(solution)/shard_map/ppermute | solution.py:110
  65.9 17.6 %collective-permute-start.13 = (bf16[256,2176]{1,0:T(8,128)(2,1)S(1)}, bf16[256,2176]{1,0:T(8,128)(2,1)S(1)}, u32[]{:S(2)}, u32[]{:S(2)}) collective-permute-start(bf16[256,2176]{1,0:T(8,128)(2,1)S(1)} %shard_map.121.x_ref.side_ref.refs_2_), channel_id=1, source_target_pairs={{0,1},{1,0},{2,3},{3,2},{4,5},{5,4},{6,7},{7,6},{8,9},{9,8},{10,11... | collective-permute-start | bytes 3342344 | tf_op jit(solution)/shard_map/ppermute | solution.py:110
  70.5 29.1 %collective-permute-start.8 = (bf16[256,2048]{1,0:T(8,128)(2,1)S(1)}, bf16[256,2048]{1,0:T(8,128)(2,1)S(1)}, u32[]{:S(2)}, u32[]{:S(2)}) collective-permute-start(bf16[256,2048]{1,0:T(8,128)(2,1)S(1)} %get-tuple-element.40), channel_id=1, source_target_pairs={{0,1},{1,0},{2,3},{3,2},{4,5},{5,4},{6,7},{7,6},{8,9},{9,8},{10,11... | collective-permute-start | bytes 3145736 | tf_op jit(solution)/shard_map/ppermute | solution.py:110
  72.9 27.0 %collective-permute-start.32 = (bf16[256,2176]{1,0:T(8,128)(2,1)S(1)}, bf16[256,2176]{1,0:T(8,128)(2,1)S(1)}, u32[]{:S(2)}, u32[]{:S(2)}) collective-permute-start(bf16[256,2176]{1,0:T(8,128)(2,1)S(1)} %get-tuple-element.50), channel_id=1, source_target_pairs={{0,1},{1,0},{2,3},{3,2},{4,5},{5,4},{6,7},{7,6},{8,9},{9,8},{10,11... | collective-permute-start | bytes 3342344 | tf_op jit(solution)/shard_map/ppermute | solution.py:110
  86.4 14.0 %collective-permute-start.14 = (bf16[256,2048]{1,0:T(8,128)(2,1)S(1)}, bf16[256,2048]{1,0:T(8,128)(2,1)S(1)}, u32[]{:S(2)}, u32[]{:S(2)}) collective-permute-start(bf16[256,2048]{1,0:T(8,128)(2,1)S(1)} %get-tuple-element.42), channel_id=1, source_target_pairs={{0,1},{1,0},{2,3},{3,2},{4,5},{5,4},{6,7},{7,6},{8,9},{9,8},{10,11... | collective-permute-start | bytes 3145736 | tf_op jit(solution)/shard_map/ppermute | solution.py:110
  88.8 15.5 %collective-permute-start.28 = (bf16[256,2176]{1,0:T(8,128)(2,1)S(1)}, bf16[256,2176]{1,0:T(8,128)(2,1)S(1)}, u32[]{:S(2)}, u32[]{:S(2)}) collective-permute-start(bf16[256,2176]{1,0:T(8,128)(2,1)S(1)} %get-tuple-element.44), channel_id=1, source_target_pairs={{0,1},{1,0},{2,3},{3,2},{4,5},{5,4},{6,7},{7,6},{8,9},{9,8},{10,11... | collective-permute-start | bytes 3342344 | tf_op jit(solution)/shard_map/ppermute | solution.py:110
  100.8 35.5 %collective-permute-start.15 = (bf16[128,2048]{1,0:T(8,128)(2,1)S(1)}, bf16[128,2048]{1,0:T(8,128)(2,1)S(1)}, u32[]{:S(2)}, u32[]{:S(2)}) collective-permute-start(bf16[128,2048]{1,0:T(8,128)(2,1)S(1)} %get-tuple-element.96), channel_id=1, source_target_pairs={{0,4},{2,6},{4,0},{6,2},{8,12},{10,14},{12,8},{14,10},{16,20},{18,... | collective-permute-start | bytes 1572872 | tf_op jit(solution)/shard_map/ppermute | solution.py:125
  102.4 34.0 %collective-permute-start.29 = (bf16[128,2048]{1,0:T(8,128)(2,1)S(1)}, bf16[128,2048]{1,0:T(8,128)(2,1)S(1)}, u32[]{:S(2)}, u32[]{:S(2)}) collective-permute-start(bf16[128,2048]{1,0:T(8,128)(2,1)S(1)} %get-tuple-element.97), channel_id=1, source_target_pairs={{0,2},{2,0},{4,6},{6,4},{8,10},{10,8},{12,14},{14,12},{16,18},{18,... | collective-permute-start | bytes 1572872 | tf_op jit(solution)/shard_map/ppermute | solution.py:125
  104.6 15.6 %collective-permute-start.44 = (bf16[32,2176]{1,0:T(8,128)(2,1)S(1)}, bf16[32,2176]{1,0:T(8,128)(2,1)S(1)}, u32[]{:S(2)}, u32[]{:S(2)}) collective-permute-start(bf16[32,2176]{1,0:T(8,128)(2,1)S(1)} %pad_maximum_fusion.16), channel_id=1, source_target_pairs={{0,2},{2,0},{4,6},{6,4},{8,10},{10,8},{12,14},{14,12},{16,18},{18,... | collective-permute-start | bytes 417800 | tf_op jit(solution)/shard_map/ppermute | solution.py:125
  104.8 12.9 %collective-permute-start.42 = (bf16[32,2176]{1,0:T(8,128)(2,1)S(1)}, bf16[32,2176]{1,0:T(8,128)(2,1)S(1)}, u32[]{:S(2)}, u32[]{:S(2)}) collective-permute-start(bf16[32,2176]{1,0:T(8,128)(2,1)S(1)} %pad_maximum_fusion.15), channel_id=1, source_target_pairs={{0,4},{2,6},{4,0},{6,2},{8,12},{10,14},{12,8},{14,10},{16,20},{18,... | collective-permute-start | bytes 417800 | tf_op jit(solution)/shard_map/ppermute | solution.py:125
  105.4 30.4 %collective-permute-start.33 = (bf16[96,2176]{1,0:T(8,128)(2,1)S(1)}, bf16[96,2176]{1,0:T(8,128)(2,1)S(1)}, u32[]{:S(2)}, u32[]{:S(2)}) collective-permute-start(bf16[96,2176]{1,0:T(8,128)(2,1)S(1)} %pad_maximum_fusion.3), channel_id=1, source_target_pairs={{0,2},{2,0},{4,6},{6,4},{8,10},{10,8},{12,14},{14,12},{16,18},{18,... | collective-permute-start | bytes 1253384 | tf_op jit(solution)/shard_map/ppermute | solution.py:125
  117.7 16.1 %collective-permute-start.46 = (bf16[96,2176]{1,0:T(8,128)(2,1)S(1)}, bf16[96,2176]{1,0:T(8,128)(2,1)S(1)}, u32[]{:S(2)}, u32[]{:S(2)}) collective-permute-start(bf16[96,2176]{1,0:T(8,128)(2,1)S(1)} %pad_maximum_fusion.4), channel_id=1, source_target_pairs={{0,4},{2,6},{4,0},{6,2},{8,12},{10,14},{12,8},{14,10},{16,20},{18,... | collective-permute-start | bytes 1253384 | tf_op jit(solution)/shard_map/ppermute | solution.py:125
  120.2 9.4 %collective-permute-start.43 = (bf16[16,2176]{1,0:T(8,128)(2,1)S(1)}, bf16[16,2176]{1,0:T(8,128)(2,1)S(1)}, u32[]{:S(2)}, u32[]{:S(2)}) collective-permute-start(bf16[16,2176]{1,0:T(8,128)(2,1)S(1)} %slice.474), channel_id=1, source_target_pairs={{0,2},{2,0},{4,6},{6,4},{8,10},{10,8},{12,14},{14,12},{16,18},{18,... | collective-permute-start | bytes 208904 | tf_op jit(solution)/shard_map/ppermute | solution.py:125
  134.0 9.7 %collective-permute-start.47 = (bf16[48,2176]{1,0:T(8,128)(2,1)S(1)}, bf16[48,2176]{1,0:T(8,128)(2,1)S(1)}, u32[]{:S(2)}, u32[]{:S(2)}) collective-permute-start(bf16[48,2176]{1,0:T(8,128)(2,1)S(1)} %slice.471), channel_id=1, source_target_pairs={{0,2},{2,0},{4,6},{6,4},{8,10},{10,8},{12,14},{14,12},{16,18},{18,... | collective-permute-start | bytes 626696 | tf_op jit(solution)/shard_map/ppermute | solution.py:125
  135.9 7.9 %collective-permute-start.34 = (bf16[48,2176]{1,0:T(8,128)(2,1)S(1)}, bf16[48,2176]{1,0:T(8,128)(2,1)S(1)}, u32[]{:S(2)}, u32[]{:S(2)}) collective-permute-start(bf16[48,2176]{1,0:T(8,128)(2,1)S(1)} %slice.472), channel_id=1, source_target_pairs={{0,4},{2,6},{4,0},{6,2},{8,12},{10,14},{12,8},{14,10},{16,20},{18,... | collective-permute-start | bytes 626696 | tf_op jit(solution)/shard_map/ppermute | solution.py:125
  136.8 4.3 %collective-permute-start.38 = (bf16[16,2048]{1,0:T(8,128)(2,1)S(1)}, bf16[16,2048]{1,0:T(8,128)(2,1)S(1)}, u32[]{:S(2)}, u32[]{:S(2)}) collective-permute-start(bf16[16,2048]{1,0:T(8,128)(2,1)S(1)} %get-tuple-element.98), channel_id=1, source_target_pairs={{0,2},{2,0},{4,6},{6,4},{8,10},{10,8},{12,14},{14,12},{16,18},{18,... | collective-permute-start | bytes 196616 | tf_op jit(solution)/shard_map/ppermute | solution.py:125
  137.2 5.7 %collective-permute-start.39 = (bf16[16,2048]{1,0:T(8,128)(2,1)S(1)}, bf16[16,2048]{1,0:T(8,128)(2,1)S(1)}, u32[]{:S(2)}, u32[]{:S(2)}) collective-permute-start(bf16[16,2048]{1,0:T(8,128)(2,1)S(1)} %get-tuple-element.103), channel_id=1, source_target_pairs={{0,4},{2,6},{4,0},{6,2},{8,12},{10,14},{12,8},{14,10},{16,20},{18,... | collective-permute-start | bytes 196616 | tf_op jit(solution)/shard_map/ppermute | solution.py:125
  139.0 24.6 %collective-permute-start.30 = (bf16[64,2048]{1,0:T(8,128)(2,1)S(1)}, bf16[64,2048]{1,0:T(8,128)(2,1)S(1)}, u32[]{:S(2)}, u32[]{:S(2)}) collective-permute-start(bf16[64,2048]{1,0:T(8,128)(2,1)S(1)} %pad_maximum_fusion.7), channel_id=1, source_target_pairs={{0,8},{2,10},{4,12},{6,14},{8,16},{10,18},{12,20},{14,22},{16,24},... | collective-permute-start | bytes 786440 | tf_op jit(solution)/shard_map/ppermute | solution.py:170
  141.2 22.4 %collective-permute-start.35 = (bf16[64,2048]{1,0:T(8,128)(2,1)S(1)}, bf16[64,2048]{1,0:T(8,128)(2,1)S(1)}, u32[]{:S(2)}, u32[]{:S(2)}) collective-permute-start(bf16[64,2048]{1,0:T(8,128)(2,1)S(1)} %pad_maximum_fusion.8), channel_id=1, source_target_pairs={{0,24},{2,26},{4,28},{6,30},{8,0},{10,2},{12,4},{14,6},{16,8},{18,... | collective-permute-start | bytes 786440 | tf_op jit(solution)/shard_map/ppermute | solution.py:170
  143.0 19.9 %collective-permute-start.40 = (bf16[32,2048]{1,0:T(8,128)(2,1)S(1)}, bf16[32,2048]{1,0:T(8,128)(2,1)S(1)}, u32[]{:S(2)}, u32[]{:S(2)}) collective-permute-start(bf16[32,2048]{1,0:T(8,128)(2,1)S(1)} %pad_maximum_fusion.22), channel_id=1, source_target_pairs={{0,16},{2,18},{4,20},{6,22},{8,24},{10,26},{12,28},{14,30},{16,0},... | collective-permute-start | bytes 393224 | tf_op jit(solution)/shard_map/ppermute | solution.py:170
  143.9 22.4 %collective-permute-start.49 = (bf16[32,2176]{1,0:T(8,128)(2,1)S(1)}, bf16[32,2176]{1,0:T(8,128)(2,1)S(1)}, u32[]{:S(2)}, u32[]{:S(2)}) collective-permute-start(bf16[32,2176]{1,0:T(8,128)(2,1)S(1)} %pad_maximum_fusion.18), channel_id=1, source_target_pairs={{0,24},{2,26},{4,28},{6,30},{8,0},{10,2},{12,4},{14,6},{16,8},{18,... | collective-permute-start | bytes 417800 | tf_op jit(solution)/shard_map/ppermute | solution.py:170
  146.0 21.4 %collective-permute-start.50 = (bf16[32,2176]{1,0:T(8,128)(2,1)S(1)}, bf16[32,2176]{1,0:T(8,128)(2,1)S(1)}, u32[]{:S(2)}, u32[]{:S(2)}) collective-permute-start(bf16[32,2176]{1,0:T(8,128)(2,1)S(1)} %pad_maximum_fusion.19), channel_id=1, source_target_pairs={{0,16},{2,18},{4,20},{6,22},{8,24},{10,26},{12,28},{14,30},{16,0},... | collective-permute-start | bytes 417800 | tf_op jit(solution)/shard_map/ppermute | solution.py:170
  162.9 6.9 %collective-permute-start.48 = (bf16[32,2176]{1,0:T(8,128)(2,1)S(1)}, bf16[32,2176]{1,0:T(8,128)(2,1)S(1)}, u32[]{:S(2)}, u32[]{:S(2)}) collective-permute-start(bf16[32,2176]{1,0:T(8,128)(2,1)S(1)} %pad_maximum_fusion.17), channel_id=1, source_target_pairs={{0,8},{2,10},{4,12},{6,14},{8,16},{10,18},{12,20},{14,22},{16,24},... | collective-permute-start | bytes 417800 | tf_op jit(solution)/shard_map/ppermute | solution.py:170
  163.8 6.2 %collective-permute-start.36 = (bf16[16,2048]{1,0:T(8,128)(2,1)S(1)}, bf16[16,2048]{1,0:T(8,128)(2,1)S(1)}, u32[]{:S(2)}, u32[]{:S(2)}) collective-permute-start(bf16[16,2048]{1,0:T(8,128)(2,1)S(1)} %get-tuple-element.110), channel_id=1, source_target_pairs={{0,2},{2,0},{4,6},{6,4},{8,10},{10,8},{12,14},{14,12},{16,18},{18,... | collective-permute-start | bytes 196616 | tf_op jit(solution)/shard_map/ppermute | solution.py:125
  165.5 4.5 %collective-permute-start.37 = (bf16[16,2048]{1,0:T(8,128)(2,1)S(1)}, bf16[16,2048]{1,0:T(8,128)(2,1)S(1)}, u32[]{:S(2)}, u32[]{:S(2)}) collective-permute-start(bf16[16,2048]{1,0:T(8,128)(2,1)S(1)} %get-tuple-element.111), channel_id=1, source_target_pairs={{0,4},{2,6},{4,0},{6,2},{8,12},{10,14},{12,8},{14,10},{16,20},{18,... | collective-permute-start | bytes 196616 | tf_op jit(solution)/shard_map/ppermute | solution.py:125
  (8 other events, 40.1 us)
